TPU v7x, 32 devices: a whole 2x2x4 slice. The times are simulated.
32 devices in a mesh: batch: 4 (over y, core), tm: 2 (over x), space: 4 (over z).
Axes of the slice: x: 2, y: 2, z: 4, core: 2. Of those that a mesh axis runs over, the one named last changes fastest.
Arguments:
- clip_tokens: bfloat16 [4, 4, 32, 32, 1024], P('batch', None, 'space', 'tm'), may hold values from -6 to 6
- frame_order: int32 [4, 4], P('batch'), may hold values from 0 to 3, each once within a row
- row_reach: int32 [4, 4], P('batch', 'tm'), may hold values from 1 to 4
- spatial_gain: float32 [1024], replicated, may hold values from 0.1 to 1.9
- spatial_heads: bfloat16 [1024, 3072], replicated, may hold values from -2 to 2
- spatial_merge: bfloat16 [1024, 1024], replicated, may hold values from -0.1875 to 0.1875
- temporal_gain: float32 [1024], replicated, may hold values from 0.1 to 1.9
- temporal_heads: bfloat16 [1024, 3072], replicated, may hold values from -2 to 2
- temporal_merge: bfloat16 [1024, 1024], replicated, may hold values from -0.1875 to 0.1875
- cotangent: bfloat16 [4, 4, 32, 32, 1024], P('batch', 'tm', 'space'), may hold values from -0.059814453 to 0.059814453
Outputs:
- output: bfloat16 [4, 4, 32, 32, 1024], P('batch', 'tm', 'space')
- weight_grad: float32 [1024, 1024], P(('tm', 'space'))
Inputs may be any that keep to these rules, and one draw needn't show every extreme that they name: Each row of frame_order names every number from 0 to 3 once.
All inputs are finite; a program needn't handle non-finite values.
Results may differ from a plain program's by a relative error of at most 0.025.
Values may be sent and summed in bfloat16 or wider, within the bound.
A program may use at most 128 MiB of HBM per device.

v0:
```python
import functools

import jax
import jax.numpy as jnp
from jax import lax
from jax.experimental import pallas as pl
from jax.experimental.pallas import tpu as pltpu
from jax.sharding import PartitionSpec as P

HALO = 4
HEADS = 16
HEAD_DIM = 64
LANES = 128
SCALE = HEAD_DIM ** (-0.5)
FLOOR = 0.5
BF = jnp.bfloat16
F32 = jnp.float32


def normalize(values, gain_vector):
    widened = values.astype(F32)
    scaled = widened * lax.rsqrt(jnp.mean(widened * widened, axis=-1, keepdims=True) + FLOOR)
    return (scaled * gain_vector).astype(BF)


def spatial_kernel(rows, cols, all_rows, reach_ref, first_ref, q_ref, k_ref, v_ref, kt_ref, vt_ref,
                   kb_ref, vb_ref, o_ref, kx, vx, bias):
    frame, block = pl.program_id(0), pl.program_id(1)
    span = HALO * cols
    window = 3 * span
    chunks = rows // HALO

    @pl.when(block == 0)
    def _():
        reach, first = reach_ref[frame], first_ref[0]
        for chunk in range(chunks):
            shape = (span, window)
            q_row = chunk * HALO + lax.broadcasted_iota(jnp.int32, shape, 0) // cols
            k_row = (chunk - 1) * HALO + lax.broadcasted_iota(jnp.int32, shape, 1) // cols
            place = first + k_row
            kept = (jnp.abs(k_row - q_row) <= reach) & (place >= 0) & (place < all_rows)
            bias[chunk] = jnp.where(kept, 0.0, -1e30)

    tokens = rows * cols
    for own, top, low, joined in ((k_ref, kt_ref, kb_ref, kx), (v_ref, vt_ref, vb_ref, vx)):
        joined[:span] = top[...]
        joined[span:span + tokens] = own[...]
        joined[span + tokens:] = low[...]

    lane = lax.broadcasted_iota(jnp.int32, (1, LANES), 1)
    first_head = (lane < HEAD_DIM).astype(F32)
    masks = (first_head.astype(BF), (1.0 - first_head).astype(BF))
    ones = jnp.ones((window, LANES), BF)
    for pair in range(q_ref.shape[1] // LANES):
        at = slice(pair * LANES, (pair + 1) * LANES)
        for chunk in range(chunks):
            here = slice(chunk * span, (chunk + 1) * span)
            near = slice(chunk * span, chunk * span + window)
            q = q_ref[here, at] * BF(SCALE)
            both = jnp.concatenate([q * masks[0], q * masks[1]], axis=0)
            s = lax.dot_general(both, kx[near, at], (((1,), (1,)), ((), ())), preferred_element_type=F32)
            s = s + jnp.concatenate([bias[chunk], bias[chunk]], axis=0)
            p = jnp.exp(s - jnp.max(s, axis=-1, keepdims=True)).astype(BF)
            o = jnp.dot(p, jnp.concatenate([vx[near, at], ones], axis=1), preferred_element_type=F32)
            o = o[:, :LANES] / o[:, LANES:]
            o_ref[here, at] = jnp.where(lane < HEAD_DIM, o[:span], o[span:]).astype(BF)


def spatial_attend(projected, halo, reach, first_row, frame, frames, rows, cols, all_rows):
    depth = projected.shape[1] // 3
    tokens, span = rows * cols, HALO * cols
    width = 2 * LANES
    blocks = depth // width
    here = lambda part: pl.BlockSpec((tokens, width), lambda f, j: (frame + f, part * blocks + j))
    beside = lambda side, part: pl.BlockSpec(
        (span, width), lambda f, j: (side * frames + frame + f, part * blocks + j))
    smem = pl.BlockSpec(memory_space=pltpu.SMEM)
    pairs = HEADS * tokens * 3 * span
    return pl.pallas_call(
        functools.partial(spatial_kernel, rows, cols, all_rows),
        grid=(1, blocks),
        out_shape=jax.ShapeDtypeStruct((tokens, depth), BF),
        in_specs=[smem, smem, here(0), here(1), here(2), beside(0, 0), beside(0, 1), beside(1, 0), beside(1, 1)],
        out_specs=pl.BlockSpec((tokens, width), lambda f, j: (f, j)),
        scratch_shapes=[
            pltpu.VMEM((tokens + 2 * span, width), BF),
            pltpu.VMEM((tokens + 2 * span, width), BF),
            pltpu.VMEM((rows // HALO, span, 3 * span), F32),
        ],
        cost_estimate=pl.CostEstimate(flops=48 * pairs * LANES, bytes_accessed=tokens * depth * 12,
                                      transcendentals=pairs),
        name="spatial",
    )(reach, first_row, projected, projected, projected, halo, halo, halo, halo)


def temporal_kernel(frames, keys, q_order, k_order, gather_ref, spread_ref, *refs):
    q_refs, k_refs, v_refs, o_ref = refs[:frames], refs[frames:frames + keys], refs[frames + keys:-1], refs[-1]
    for f in range(frames):
        q = q_refs[f][...] * BF(SCALE)
        scores = []
        for g in range(keys):
            s = jnp.dot(q * k_refs[g][...], gather_ref[...], preferred_element_type=F32)
            scores.append(s + jnp.where(k_order[g] <= q_order[f], 0.0, -1e30))
        top_score = functools.reduce(jnp.maximum, scores)
        exps = [jnp.exp(s - top_score) for s in scores]
        scale = 1.0 / functools.reduce(jnp.add, exps)
        total = None
        for g in range(keys):
            w = jnp.dot((exps[g] * scale).astype(BF), spread_ref[...], preferred_element_type=F32)
            term = w * v_refs[g][...].astype(F32)
            total = term if total is None else total + term
        o_ref[f] = total.astype(BF)


def temporal_attend(own, others, q_order, k_order):
    frames, keys = len(own), len(own) + len(others)
    tokens, depth = own[0].shape[0], own[0].shape[1] // 3
    size = min(tokens, 64)
    head = jnp.arange(depth, dtype=jnp.int32) // HEAD_DIM
    gather = (head[:, None] == jnp.arange(LANES, dtype=jnp.int32)[None, :]).astype(BF)
    part = lambda column: pl.BlockSpec((size, depth), lambda i: (i, column))
    smem = pl.BlockSpec(memory_space=pltpu.SMEM)
    whole = lambda shape: pl.BlockSpec(shape, lambda i: (0, 0))
    out = pl.pallas_call(
        functools.partial(temporal_kernel, frames, keys),
        grid=(tokens // size,),
        out_shape=jax.ShapeDtypeStruct((frames, tokens, depth), BF),
        in_specs=[smem, smem, whole((depth, LANES)), whole((LANES, depth))] + [part(0)] * frames
        + [part(1)] * frames + [part(0)] * len(others) + [part(2)] * frames + [part(1)] * len(others),
        out_specs=pl.BlockSpec((frames, size, depth), lambda i: (0, i, 0)),
        cost_estimate=pl.CostEstimate(flops=4 * frames * keys * tokens * depth * LANES,
                                      bytes_accessed=4 * keys * tokens * depth, transcendentals=0),
        name="temporal",
    )(q_order, k_order, gather, gather.T, *own, *own, *others, *own, *others)
    return out.reshape(frames * tokens, depth)


def cyclic(axis, shift):
    n = lax.axis_size(axis)
    return [(i, (i + shift) % n) for i in range(n)]


def exchange_bit(value, axis, bit):
    n = lax.axis_size(axis)
    return lax.ppermute(value, axis, [(i, i ^ bit) for i in range(n)])


def halve_columns(value, bit):
    half = value.shape[1] // 2
    mine = lax.axis_index("batch") // bit % 2
    sent = lax.dynamic_slice_in_dim(value, (1 - mine) * half, half, 1)
    kept = lax.dynamic_slice_in_dim(value, mine * half, half, 1)
    arrived = exchange_bit(sent, "batch", bit)
    return (kept.astype(F32) + arrived.astype(F32)).astype(BF)


def scatter_rows(value, axis):
    n, me = lax.axis_size(axis), lax.axis_index(axis)
    size = value.shape[0] // n
    take = lambda owner: lax.dynamic_slice_in_dim(value, owner * size, size, 0)
    total = take(me).astype(F32)
    for shift in range(1, n):
        arrived = lax.ppermute(take((me + shift) % n), axis, cyclic(axis, shift))
        total = total + arrived.astype(F32)
    return total.astype(BF)


def reduce_gradient(part):
    n, me = lax.axis_size("batch"), lax.axis_index("batch")
    bits = [1 << i for i in range(n.bit_length() - 1)]
    part = halve_columns(part, bits[0])
    half = part.shape[1] // 2
    one, two = part[:, :half], part[:, half:]
    for bit in bits[1:]:
        one = halve_columns(one, bit)
    two = scatter_rows(two, "tm")
    one = scatter_rows(one, "tm")
    for bit in bits[1:]:
        two = halve_columns(two, bit)
    piece = scatter_rows(jnp.concatenate([one, two], axis=1), "space")
    pieces = [piece] + [exchange_bit(piece, "batch", d) for d in range(1, n)]
    placed = [lax.select_n(me ^ b, *pieces) for b in range(n)]
    small = piece.shape[1] // 2

    def ordered(prefix, left):
        if not left:
            return [placed[prefix]]
        return ordered(prefix, left[1:]) + ordered(prefix + left[0], left[1:])

    columns = []
    for first in (0, bits[0]):
        owners = ordered(first, bits[1:])
        columns += [owner[:, :small] for owner in owners] + [owner[:, small:] for owner in owners]
    return jnp.concatenate(columns, axis=1).astype(F32)


def per_device(clip_tokens, frame_order, row_reach, spatial_gain, spatial_heads, spatial_merge,
               temporal_gain, temporal_heads, temporal_merge, cotangent):
    ranks, me = lax.axis_size("tm"), lax.axis_index("tm")
    places, place = lax.axis_size("space"), lax.axis_index("space")
    _, all_frames, rows, part_cols, depth = clip_tokens.shape
    frames, cols = all_frames // ranks, part_cols * ranks
    tokens, span = rows * cols, HALO * cols
    clip = clip_tokens[0]
    up = [(i, i + 1) for i in range(places - 1)]
    down = [(i + 1, i) for i in range(places - 1)]
    first_row = (place * rows).astype(jnp.int32).reshape(1)
    reach = row_reach.reshape(-1)

    def project(values, gain, weights):
        return jnp.dot(normalize(values, gain), weights, preferred_element_type=F32).astype(BF)

    pieces = []
    for shift in range(ranks):
        block = lax.dynamic_slice_in_dim(clip, (me + shift) % ranks * frames, frames, 0)
        pieces.append(lax.ppermute(block, "tm", cyclic("tm", shift)) if shift else block)
    here = jnp.stack([lax.select_n((me - j) % ranks, *pieces) if ranks > 2 else
                      jnp.where(me == j, pieces[0], pieces[1]) for j in range(ranks)], axis=2)
    here = here.reshape(frames, rows, cols, depth)
    above = lax.ppermute(here[:, rows - HALO:], "space", up).reshape(frames * span, depth)
    below = lax.ppermute(here[:, :HALO], "space", down).reshape(frames * span, depth)
    flat = here.reshape(frames * tokens, depth)
    projected = project(flat, spatial_gain, spatial_heads)
    halo = project(jnp.concatenate([above, below]), spatial_gain, spatial_heads[:, depth:])
    middles = []
    for f in range(frames):
        reach_now = reach[f:f + 1]
        if f:
            middles[-1], reach_now = lax.optimization_barrier((middles[-1], reach_now))
        context = spatial_attend(projected, halo, reach_now, first_row, f, frames, rows, cols, rows * places)
        middles.append((flat[f * tokens:(f + 1) * tokens].astype(F32)
                        + jnp.dot(context, spatial_merge, preferred_element_type=F32)).astype(BF))

    order = frame_order.reshape(-1)
    orders = [lax.dynamic_slice_in_dim(order, (me - shift) % ranks * frames, frames, 0) for shift in range(ranks)]
    arrived = [lax.ppermute(value, "tm", cyclic("tm", shift)) for shift in range(1, ranks) for value in middles]
    own = [project(value, temporal_gain, temporal_heads) for value in middles]
    others = [project(value, temporal_gain, temporal_heads[:, depth:]) for value in arrived]
    context = temporal_attend(own, others, orders[0], jnp.concatenate(orders))
    middle = jnp.concatenate(middles)
    part = lax.dot_general(context, cotangent.reshape(-1, depth), (((0,), (0,)), ((), ())),
                           preferred_element_type=F32).astype(BF)
    weight_grad = reduce_gradient(part)
    output = (middle.astype(F32) + jnp.dot(context, temporal_merge, preferred_element_type=F32)).astype(BF)
    return output.reshape(1, frames, rows, cols, depth), weight_grad


def solution(mesh):
    in_specs = (
        P("batch", None, "space", "tm", None),
        P("batch", None),
        P("batch", "tm"),
        P(),
        P(),
        P(),
        P(),
        P(),
        P(),
        P("batch", "tm", "space", None, None),
    )
    out_specs = (P("batch", "tm", "space", None, None), P(("tm", "space"), None))
    return jax.shard_map(per_device, mesh=mesh, in_specs=in_specs, out_specs=out_specs, check_vma=False)
```

profile of v0, /device:TPU:0, one launch (start us, length us, event | category | flops | bytes accessed | tf_op | source)
XLA Modules:
  0.0 131.0 jit_solution(8240557996829528485)
XLA Ops:
  0.7 1.2 dynamic-slice_bitcast_fusion
  1.9 3.0 %collective-permute-start = (bf16[2,8,16,1024]{3,2,1,0:T(8,128)(2,1)S(1)}, bf16[2,8,16,1024]{3,2,1,0:T(8,128)(2,1)}, u32[]{:S(2)}, u32[]{:S(2)}) collective-permute-start(bf16[2,8,16,1024]{3,2,1,0:T(8,128)(2,1)S(1)} %dynamic-slice_bitcast_fusion), channel_id=1, source_target_pairs={{0,4},{4,0},{1,5},{5,1},{2,6},{6,2},{3,7},{7,3},{8,12},{12,8},{9,1... | collective-permute-start | bytes 1572872 | tf_op jit(solution)/shard_map/ppermute | solution.py:216
  4.9 1.3 %fusion.67 = (s32[1,1]{1,0:T(1,128)}, s32[1,1]{1,0:T(1,128)}) fusion(s32[1,2]{1,0:T(1,128)} %param.12), kind=kLoop, calls=%fused_computation.130 | loop fusion | bytes 16 | tf_op jit(solution)/shard_map/slice | solution.py:227
  6.3 0.8 fusion.63
  7.1 0.6 pad_add_fusion.k_order
  7.7 0.9 fusion.53.gather_ref
  8.6 0.8 fusion.54.spread_ref
  9.4 7.6 %collective-permute-done = bf16[2,8,16,1024]{3,2,1,0:T(8,128)(2,1)} collective-permute-done((bf16[2,8,16,1024]{3,2,1,0:T(8,128)(2,1)S(1)}, bf16[2,8,16,1024]{3,2,1,0:T(8,128)(2,1)}, u32[]{:S(2)}, u32[]{:S(2)}) %collective-permute-start) | collective-permute-done | bytes 524320 | tf_op jit(solution)/shard_map/ppermute | solution.py:216
  17.0 1.3 fusion.43
  18.6 1.1 fusion.42
  19.7 1.1 fusion.66
  20.8 4.5 %collective-permute-start.1 = (bf16[2,4,32,1024]{3,2,1,0:T(8,128)(2,1)}, bf16[2,4,32,1024]{3,2,1,0:T(8,128)(2,1)}, u32[]{:S(2)}, u32[]{:S(2)}) collective-permute-start(bf16[2,4,32,1024]{3,2,1,0:T(8,128)(2,1)} %get-tuple-element.14), channel_id=1, source_target_pairs={{0,1},{1,2},{2,3},{4,5},{5,6},{6,7},{8,9},{9,10},{10,11},{12,13},{... | collective-permute-start | bytes 1572872 | tf_op jit(solution)/shard_map/ppermute | solution.py:220
  25.3 1.3 collective-permute-start.2
  27.0 7.7 %convolution_convert_fusion.q_ref.k_ref.v_ref = bf16[512,3072]{1,0:T(8,128)(2,1)} fusion(bf16[512,1024]{1,0:T(8,128)(2,1)S(1)} %fusion.19, bf16[1024,3072]{1,0:T(8,128)(2,1)} %param.14), kind=kOutput, calls=%fused_computation | convolution fusion | flops 3222798336 | bytes 10485760 | tf_op jit(solution)/shard_map/dot_general | solution.py:211
  35.1 4.9 %collective-permute-done.2 = bf16[2,4,32,1024]{3,2,1,0:T(8,128)(2,1)} collective-permute-done((bf16[2,4,32,1024]{3,2,1,0:T(8,128)(2,1)}, bf16[2,4,32,1024]{3,2,1,0:T(8,128)(2,1)}, u32[]{:S(2)}, u32[]{:S(2)}) %collective-permute-start.2) | collective-permute-done | bytes 524320 | tf_op jit(solution)/shard_map/ppermute | solution.py:221
  40.0 1.5 %fusion.15 = f32[512]{0:T(512)S(1)} fusion(bf16[256,1024]{1,0:T(8,128)(2,1)} %bitcast.11, bf16[256,1024]{1,0:T(8,128)(2,1)} %bitcast.10), kind=kLoop, calls=%fused_computation.14 | loop fusion | flops 3145216 | bytes 1050624 | tf_op jit(solution)/shard_map/reduce_sum | solution.py:22
  41.5 5.0 %fusion.6.kt_ref.vt_ref.kb_ref.vb_ref = bf16[512,2048]{1,0:T(8,128)(2,1)} fusion(bf16[1024,3072]{1,0:T(8,128)(2,1)S(1)} %bitcast.56, f32[512]{0:T(512)S(1)} %add_rsqrt_fusion.1, f32[1024]{0:T(1024)S(1)} %copy-done.4, bf16[256,1024]{1,0:T(8,128)(2,1)} %bitcast.11, bf16[256,1024]{1,0:T(8,128)(2,1)} %bitcast.10), kind=kOutput, calls=%fused_computation.9 | convolution fusion | flops 2152202240 | bytes 7346176 | tf_op jit(solution)/shard_map/dot_general | solution.py:211
  46.6 7.1 %spatial.2 = bf16[256,1024]{1,0:T(8,128)(2,1)} custom-call(s32[1]{0:T(128)} %bitcast.6.reach_ref, s32[1]{0:T(128)} %bitcast.7.first_ref, bf16[512,3072]{1,0:T(8,128)(2,1)} %convolution_convert_fusion.q_ref.k_ref.v_ref, bf16[512,3072]{1,0:T(8,128)(2,1)} %convolution_convert_fusion.q_ref.k_ref.v_ref, ...), custom_call_target="tpu_custom_call" | custom-call | flops 9663676416 | bytes 3145728 | tf_op jit(solution)/shard_map/spatial/pallas_call | solution.py:79
  53.7 1.8 %fusion.20 = bf16[256,1024]{1,0:T(8,128)(2,1)S(1)} fusion(bf16[256,1024]{1,0:T(8,128)(2,1)} %spatial.2, bf16[1024,1024]{1,0:T(8,128)(2,1)S(1)} %copy-done, bf16[256,1024]{1,0:T(8,128)(2,1)S(1)} %bitcast.54), kind=kOutput, calls=%fused_computation.39 | convolution fusion | flops 537657344 | bytes 3670016 | tf_op jit(solution)/shard_map/dot_general | solution.py:232
  55.5 1.6 %collective-permute-start.3 = (bf16[256,1024]{1,0:T(8,128)(2,1)S(1)}, bf16[256,1024]{1,0:T(8,128)(2,1)S(1)}, u32[]{:S(2)}, u32[]{:S(2)}) collective-permute-start(bf16[256,1024]{1,0:T(8,128)(2,1)S(1)} %fusion.20), channel_id=1, source_target_pairs={{0,4},{4,0},{1,5},{5,1},{2,6},{6,2},{3,7},{7,3},{8,12},{12,8},{9,1... | collective-permute-start | bytes 1572872 | tf_op jit(solution)/shard_map/ppermute | solution.py:236
  57.2 7.1 %spatial.3 = bf16[256,1024]{1,0:T(8,128)(2,1)} custom-call(s32[1]{0:T(128)} %bitcast.12.reach_ref, s32[1]{0:T(128)} %bitcast.7.first_ref, bf16[512,3072]{1,0:T(8,128)(2,1)} %convolution_convert_fusion.q_ref.k_ref.v_ref, bf16[512,3072]{1,0:T(8,128)(2,1)} %convolution_convert_fusion.q_ref.k_ref.v_ref, ...), custom_call_target="tpu_custom_call" | custom-call | flops 9663676416 | bytes 3145728 | tf_op jit(solution)/shard_map/spatial/pallas_call | solution.py:79
  64.3 2.2 %fusion.25 = (f32[256]{0:T(256)S(1)}, bf16[256,1024]{1,0:T(8,128)(2,1)S(1)}) fusion(bf16[256,1024]{1,0:T(8,128)(2,1)} %spatial.3, bf16[1024,1024]{1,0:T(8,128)(2,1)S(1)} %copy-done, bf16[256,1024]{1,0:T(8,128)(2,1)} %bitcast.53), kind=kOutput, calls=%fused_computation.44 | convolution fusion | flops 538443520 | bytes 3671040 | tf_op jit(solution)/shard_map/dot_general | solution.py:232
  67.1 6.0 %convolution_convert_fusion.1.refs_1_.refs_3_.refs_7_ = bf16[256,3072]{1,0:T(8,128)(2,1)} fusion(bf16[1024,3072]{1,0:T(8,128)(2,1)} %param.17, bf16[256,1024]{1,0:T(8,128)(2,1)S(1)} %get-tuple-element.28, f32[256]{0:T(256)S(1)} %add_rsqrt_fusion.4, f32[1024]{0:T(1024)S(1)} %copy-done.8), kind=kOutput, calls=%fused_computation.3 | convolution fusion | flops 1612447744 | bytes 8393728 | tf_op jit(solution)/shard_map/dot_general | solution.py:211
  73.1 3.1 %convolution_convert_fusion.2.refs_0_.refs_2_.refs_6_ = bf16[256,3072]{1,0:T(8,128)(2,1)} fusion(bf16[1024,3072]{1,0:T(8,128)(2,1)S(1)} %bitcast.58, bf16[256,1024]{1,0:T(8,128)(2,1)S(1)} %fusion.20, f32[1024]{0:T(1024)S(1)} %copy-done.8, f32[256]{0:T(256)S(1)} %add_rsqrt_fusion.5), kind=kOutput, calls=%fused_computation.4 | convolution fusion | flops 1612447744 | bytes 8393728 | tf_op jit(solution)/shard_map/dot_general | solution.py:211
  76.2 2.3 %collective-permute-done.4 = bf16[256,1024]{1,0:T(8,128)(2,1)S(1)} collective-permute-done((bf16[256,1024]{1,0:T(8,128)(2,1)S(1)}, bf16[256,1024]{1,0:T(8,128)(2,1)S(1)}, u32[]{:S(2)}, u32[]{:S(2)}) %collective-permute-start.4) | collective-permute-done | bytes 524320 | tf_op jit(solution)/shard_map/ppermute | solution.py:236
  78.9 2.4 %fusion.12.refs_5_.refs_9_ = bf16[256,2048]{1,0:T(8,128)(2,1)} fusion(bf16[1024,3072]{1,0:T(8,128)(2,1)S(1)} %bitcast.58, bf16[256,1024]{1,0:T(8,128)(2,1)S(1)} %collective-permute-done.4, f32[256]{0:T(256)S(1)} %add_rsqrt_fusion.2, f32[1024]{0:T(1024)S(1)} %copy-done.8), kind=kOutput, calls=%fused_computation.13 | convolution fusion | flops 1075314688 | bytes 5772288 | tf_op jit(solution)/shard_map/dot_general | solution.py:211
  81.2 2.3 %fusion.9.refs_4_.refs_8_ = bf16[256,2048]{1,0:T(8,128)(2,1)} fusion(bf16[1024,3072]{1,0:T(8,128)(2,1)S(1)} %bitcast.58, bf16[256,1024]{1,0:T(8,128)(2,1)S(1)} %collective-permute-done.3, f32[256]{0:T(256)S(1)} %add_rsqrt_fusion.3, f32[1024]{0:T(1024)S(1)} %copy-done.8), kind=kOutput, calls=%fused_computation.12 | convolution fusion | flops 1075314688 | bytes 5772288 | tf_op jit(solution)/shard_map/dot_general | solution.py:211
  83.6 7.3 %temporal.1 = bf16[2,256,1024]{2,1,0:T(8,128)(2,1)} custom-call(s32[2]{0:T(128)} %copy-done.5, s32[4]{0:T(128)} %pad_add_fusion.k_order, bf16[1024,128]{1,0:T(8,128)(2,1)} %fusion.53.gather_ref, bf16[128,1024]{1,0:T(8,128)(2,1)} %fusion.54.spread_ref, bf16[256,3072]{1,0:T(8,128)(2,1)} %convolution_convert_fusion.2.refs_0_.refs_2_.refs_6_, ...), custom_call_target="tpu_custom_call" | custom-call | flops 1073741824 | bytes 4194304 | tf_op jit(solution)/shard_map/temporal/pallas_call | solution.py:124
  90.9 2.5 %convolution_convert_fusion.3 = bf16[1024,1024]{0,1:T(8,128)(2,1)S(1)} fusion(bf16[512,1024]{1,0:T(8,128)(2,1)} %bitcast.51, bf16[512,1024]{1,0:T(8,128)(2,1)S(1)} %bitcast.59), kind=kOutput, calls=%fused_computation.23 | convolution fusion | flops 1074790400 | bytes 4194304 | tf_op jit(solution)/shard_map/dot_general | solution.py:241
  93.4 1.3 %copy-done.1 = bf16[1024,1024]{0,1:T(8,128)(2,1)} copy-done((bf16[1024,1024]{0,1:T(8,128)(2,1)}, bf16[1024,1024]{0,1:T(8,128)(2,1)S(1)}, u32[]{:S(2)}) %copy-start.1) | copy-done | bytes 2097176
  94.9 2.8 %collective-permute-done.5 = bf16[1024,512]{0,1:T(8,128)(2,1)} collective-permute-done((bf16[1024,512]{0,1:T(8,128)(2,1)S(1)}, bf16[1024,512]{0,1:T(8,128)(2,1)}, u32[]{:S(2)}, u32[]{:S(2)}) %collective-permute-start.5) | collective-permute-done | bytes 1048608 | tf_op jit(solution)/shard_map/ppermute | solution.py:145
  97.7 1.9 %add_convert_fusion = bf16[1024,512]{0,1:T(8,128)(2,1)S(1)} fusion(bf16[1024,512]{0,1:T(8,128)(2,1)} %collective-permute-done.5, bf16[1024,1024]{0,1:T(8,128)(2,1)} %copy-done.1, s32[]{:T(128)S(6)} %select_n.242), kind=kLoop, calls=%fused_computation.20 | loop fusion | flops 2097152 | bytes 3145732 | tf_op jit(solution)/shard_map/convert_element_type | solution.py:154
  99.7 1.6 %collective-permute-start.8 = (bf16[512,256]{0,1:T(8,128)(2,1)S(1)}, bf16[512,256]{0,1:T(8,128)(2,1)}, u32[]{:S(2)}, u32[]{:S(2)}) collective-permute-start(bf16[512,256]{0,1:T(8,128)(2,1)S(1)} %constant_dynamic-slice_fusion.1), channel_id=1, source_target_pairs={{0,4},{4,0},{1,5},{5,1},{2,6},{6,2},{3,7},{7,3},{8,12},{12,8},{9,1... | collective-permute-start | bytes 786440 | tf_op jit(solution)/shard_map/ppermute | solution.py:163
  101.3 1.6 %collective-permute-start.6 = (bf16[1024,128]{0,1:T(8,128)(2,1)S(1)}, bf16[1024,128]{0,1:T(8,128)(2,1)S(1)}, u32[]{:S(2)}, u32[]{:S(2)}) collective-permute-start(bf16[1024,128]{0,1:T(8,128)(2,1)S(1)} %constant_dynamic-slice_fusion.3), channel_id=1, source_target_pairs={{0,16},{8,24},{16,0},{24,8},{1,17},{9,25},{17,1},{25,9},{2,18},{10... | collective-permute-start | bytes 786440 | tf_op jit(solution)/shard_map/ppermute | solution.py:145
  102.9 5.4 %collective-permute-done.8 = bf16[512,256]{0,1:T(8,128)(2,1)} collective-permute-done((bf16[512,256]{0,1:T(8,128)(2,1)S(1)}, bf16[512,256]{0,1:T(8,128)(2,1)}, u32[]{:S(2)}, u32[]{:S(2)}) %collective-permute-start.8) | collective-permute-done | bytes 262176 | tf_op jit(solution)/shard_map/ppermute | solution.py:163
  108.2 1.0 add_convert_fusion.2
  109.3 1.6 %collective-permute-start.9 = (bf16[512,128]{0,1:T(8,128)(2,1)S(1)}, bf16[512,128]{0,1:T(8,128)(2,1)S(1)}, u32[]{:S(2)}, u32[]{:S(2)}) collective-permute-start(bf16[512,128]{0,1:T(8,128)(2,1)S(1)} %constant_dynamic-slice_fusion), channel_id=1, source_target_pairs={{0,16},{8,24},{16,0},{24,8},{1,17},{9,25},{17,1},{25,9},{2,18},{10... | collective-permute-start | bytes 393224 | tf_op jit(solution)/shard_map/ppermute | solution.py:145
  111.0 1.5 %collective-permute-start.7 = (bf16[512,128]{0,1:T(8,128)(2,1)S(1)}, bf16[512,128]{0,1:T(8,128)(2,1)S(1)}, u32[]{:S(2)}, u32[]{:S(2)}) collective-permute-start(bf16[512,128]{0,1:T(8,128)(2,1)S(1)} %constant_dynamic-slice_fusion.2), channel_id=1, source_target_pairs={{0,4},{4,0},{1,5},{5,1},{2,6},{6,2},{3,7},{7,3},{8,12},{12,8},{9,1... | collective-permute-start | bytes 393224 | tf_op jit(solution)/shard_map/ppermute | solution.py:163
  112.5 1.8 %collective-permute-done.9 = bf16[512,128]{0,1:T(8,128)(2,1)S(1)} collective-permute-done((bf16[512,128]{0,1:T(8,128)(2,1)S(1)}, bf16[512,128]{0,1:T(8,128)(2,1)S(1)}, u32[]{:S(2)}, u32[]{:S(2)}) %collective-permute-start.9) | collective-permute-done | bytes 131104 | tf_op jit(solution)/shard_map/ppermute | solution.py:145
  114.4 1.7 %collective-permute-done.7 = bf16[512,128]{0,1:T(8,128)(2,1)S(1)} collective-permute-done((bf16[512,128]{0,1:T(8,128)(2,1)S(1)}, bf16[512,128]{0,1:T(8,128)(2,1)S(1)}, u32[]{:S(2)}, u32[]{:S(2)}) %collective-permute-start.7) | collective-permute-done | bytes 131104 | tf_op jit(solution)/shard_map/ppermute | solution.py:163
  116.1 0.9 collective-permute-start.10
  117.0 1.1 collective-permute-start.11
  118.1 2.8 %collective-permute-start.12 = (bf16[128,256]{0,1:T(8,128)(2,1)S(1)}, bf16[128,256]{0,1:T(8,128)(2,1)S(1)}, u32[]{:S(2)}, u32[]{:S(2)}) collective-permute-start(bf16[128,256]{0,1:T(8,128)(2,1)S(1)} %get-tuple-element.22), channel_id=1, source_target_pairs={{0,3},{1,0},{2,1},{3,2},{4,7},{5,4},{6,5},{7,6},{8,11},{9,8},{10,9... | collective-permute-start | bytes 196616 | tf_op jit(solution)/shard_map/ppermute | solution.py:163
  120.9 1.5 %collective-permute-done.10 = bf16[128,256]{0,1:T(8,128)(2,1)S(1)} collective-permute-done((bf16[128,256]{0,1:T(8,128)(2,1)S(1)}, bf16[128,256]{0,1:T(8,128)(2,1)S(1)}, u32[]{:S(2)}, u32[]{:S(2)}) %collective-permute-start.10) | collective-permute-done | bytes 65568 | tf_op jit(solution)/shard_map/ppermute | solution.py:163
  122.4 1.2 collective-permute-done.11
  124.2 1.3 collective-permute-start.15
  125.5 4.4 %add_convert_fusion.1 = bf16[512,1024]{1,0:T(8,128)(2,1)} fusion(bf16[512,1024]{1,0:T(8,128)(2,1)} %bitcast.52, bf16[1024,1024]{1,0:T(8,128)(2,1)} %param.18, bf16[256,1024]{1,0:T(8,128)(2,1)} %copy-done.7, bf16[256,1024]{1,0:T(8,128)(2,1)} %copy-done.2), kind=kOutput, calls=%fused_computation.21 | convolution fusion | flops 1076887552 | bytes 5242880 | tf_op jit(solution)/shard_map/dot_general | solution.py:244
  130.1 0.9 copy.13
  (72 shorter events, 3.7 us)
Async XLA Ops:
  0.6 53.1 %copy-start = (bf16[1024,1024]{1,0:T(8,128)(2,1)S(1)}, bf16[1024,1024]{1,0:T(8,128)(2,1)}, u32[]{:S(2)}) copy-start(bf16[1024,1024]{1,0:T(8,128)(2,1)} %param.15) | copy-start | bytes 6291460
  1.9 15.1 %collective-permute-start = (bf16[2,8,16,1024]{3,2,1,0:T(8,128)(2,1)S(1)}, bf16[2,8,16,1024]{3,2,1,0:T(8,128)(2,1)}, u32[]{:S(2)}, u32[]{:S(2)}) collective-permute-start(bf16[2,8,16,1024]{3,2,1,0:T(8,128)(2,1)S(1)} %dynamic-slice_bitcast_fusion), channel_id=1, source_target_pairs={{0,4},{4,0},{1,5},{5,1},{2,6},{6,2},{3,7},{7,3},{8,12},{12,8},{9,1... | collective-permute-start | bytes 1572872 | tf_op jit(solution)/shard_map/ppermute | solution.py:216
  7.1 11.3 %copy-start.5 = (s32[2]{0:T(128)}, s32[2]{0:T(128)S(1)}, u32[]{:S(2)}) copy-start(s32[2]{0:T(128)S(1)} %get-tuple-element.26.q_order) | copy-start | bytes 28
  18.6 8.1 %copy-start.4 = (f32[1024]{0:T(1024)S(1)}, f32[1024]{0:T(1024)}, u32[]{:S(2)}) copy-start(f32[1024]{0:T(1024)} %param.13) | copy-start | bytes 12292
  20.8 14.4 %collective-permute-start.1 = (bf16[2,4,32,1024]{3,2,1,0:T(8,128)(2,1)}, bf16[2,4,32,1024]{3,2,1,0:T(8,128)(2,1)}, u32[]{:S(2)}, u32[]{:S(2)}) collective-permute-start(bf16[2,4,32,1024]{3,2,1,0:T(8,128)(2,1)} %get-tuple-element.14), channel_id=1, source_target_pairs={{0,1},{1,2},{2,3},{4,5},{5,6},{6,7},{8,9},{9,10},{10,11},{12,13},{... | collective-permute-start | bytes 1572872 | tf_op jit(solution)/shard_map/ppermute | solution.py:220
  25.3 14.7 %collective-permute-start.2 = (bf16[2,4,32,1024]{3,2,1,0:T(8,128)(2,1)}, bf16[2,4,32,1024]{3,2,1,0:T(8,128)(2,1)}, u32[]{:S(2)}, u32[]{:S(2)}) collective-permute-start(bf16[2,4,32,1024]{3,2,1,0:T(8,128)(2,1)} %get-tuple-element.15), channel_id=1, source_target_pairs={{1,0},{2,1},{3,2},{5,4},{6,5},{7,6},{9,8},{10,9},{11,10},{13,12},{... | collective-permute-start | bytes 1572872 | tf_op jit(solution)/shard_map/ppermute | solution.py:221
  26.7 14.8 %slice-start = ((s8[6291456]{0:T(1024)(128)(4,1)}), s8[4194304]{0:T(1024)(128)(4,1)S(1)}, s32[]{:S(2)}) async-start(s8[6291456]{0:T(1024)(128)(4,1)} %bitcast.55), calls=%async_computation | async-start | bytes 8388608
  27.0 14.5 %slice-start.1 = ((s8[6291456]{0:T(1024)(128)(4,1)}), s8[2097152]{0:T(1024)(128)(4,1)S(1)}, s32[]{:S(2)}) async-start(s8[6291456]{0:T(1024)(128)(4,1)} %bitcast.55), calls=%async_computation.1 | async-start | bytes 4194304
  46.6 7.1 %copy-start.3 = (bf16[1,8,2,16,1024]{4,3,2,1,0:T(8,128)(2,1)S(1)}, bf16[1,8,2,16,1024]{4,3,2,1,0:T(8,128)(2,1)}, u32[]{:S(2)}) copy-start(bf16[1,8,2,16,1024]{4,3,2,1,0:T(8,128)(2,1)} %get-tuple-element.13) | copy-start | bytes 1572868
  55.5 17.6 %copy-start.2 = (bf16[256,1024]{1,0:T(8,128)(2,1)}, bf16[256,1024]{1,0:T(8,128)(2,1)S(1)}, u32[]{:S(2)}) copy-start(bf16[256,1024]{1,0:T(8,128)(2,1)S(1)} %fusion.20) | copy-start | bytes 1572868
  55.5 23.2 %collective-permute-start.3 = (bf16[256,1024]{1,0:T(8,128)(2,1)S(1)}, bf16[256,1024]{1,0:T(8,128)(2,1)S(1)}, u32[]{:S(2)}, u32[]{:S(2)}) collective-permute-start(bf16[256,1024]{1,0:T(8,128)(2,1)S(1)} %fusion.20), channel_id=1, source_target_pairs={{0,4},{4,0},{1,5},{5,1},{2,6},{6,2},{3,7},{7,3},{8,12},{12,8},{9,1... | collective-permute-start | bytes 1572872 | tf_op jit(solution)/shard_map/ppermute | solution.py:236
  64.3 2.8 %copy-start.8 = (f32[1024]{0:T(1024)S(1)}, f32[1024]{0:T(1024)}, u32[]{:S(2)}) copy-start(f32[1024]{0:T(1024)} %param.16) | copy-start | bytes 12292
  64.3 8.8 %slice-start.2 = ((s8[6291456]{0:T(1024)(128)(4,1)}), s8[4194304]{0:T(1024)(128)(4,1)S(1)}, s32[]{:S(2)}) async-start(s8[6291456]{0:T(1024)(128)(4,1)} %bitcast.57), calls=%async_computation.2 | async-start | bytes 8388608
  66.5 6.6 %copy-start.7 = (bf16[256,1024]{1,0:T(8,128)(2,1)}, bf16[256,1024]{1,0:T(8,128)(2,1)S(1)}, u32[]{:S(2)}) copy-start(bf16[256,1024]{1,0:T(8,128)(2,1)S(1)} %get-tuple-element.28) | copy-start | bytes 1572868
  66.5 12.0 %collective-permute-start.4 = (bf16[256,1024]{1,0:T(8,128)(2,1)S(1)}, bf16[256,1024]{1,0:T(8,128)(2,1)S(1)}, u32[]{:S(2)}, u32[]{:S(2)}) collective-permute-start(bf16[256,1024]{1,0:T(8,128)(2,1)S(1)} %get-tuple-element.28), channel_id=1, source_target_pairs={{0,4},{4,0},{1,5},{5,1},{2,6},{6,2},{3,7},{7,3},{8,12},{12,8},{9,1... | collective-permute-start | bytes 1572872 | tf_op jit(solution)/shard_map/ppermute | solution.py:236
  67.1 6.0 %slice-start.3 = ((s8[6291456]{0:T(1024)(128)(4,1)}), s8[2097152]{0:T(1024)(128)(4,1)S(1)}, s32[]{:S(2)}) async-start(s8[6291456]{0:T(1024)(128)(4,1)} %bitcast.57), calls=%async_computation.3 | async-start | bytes 4194304
  83.5 7.3 %copy-start.6 = (bf16[1,2,8,32,1024]{4,3,2,1,0:T(8,128)(2,1)S(1)}, bf16[1,2,8,32,1024]{4,3,2,1,0:T(8,128)(2,1)}, u32[]{:S(2)}) copy-start(bf16[1,2,8,32,1024]{4,3,2,1,0:T(8,128)(2,1)} %param.19) | copy-start | bytes 3145732
  93.4 1.3 %copy-start.1 = (bf16[1024,1024]{0,1:T(8,128)(2,1)}, bf16[1024,1024]{0,1:T(8,128)(2,1)S(1)}, u32[]{:S(2)}) copy-start(bf16[1024,1024]{0,1:T(8,128)(2,1)S(1)} %convolution_convert_fusion.3) | copy-start | bytes 6291460
  94.8 2.9 %collective-permute-start.5 = (bf16[1024,512]{0,1:T(8,128)(2,1)S(1)}, bf16[1024,512]{0,1:T(8,128)(2,1)}, u32[]{:S(2)}, u32[]{:S(2)}) collective-permute-start(bf16[1024,512]{0,1:T(8,128)(2,1)S(1)} %constant_dynamic-slice_fusion.4), channel_id=1, source_target_pairs={{0,8},{8,0},{16,24},{24,16},{1,9},{9,1},{17,25},{25,17},{2,10},{10... | collective-permute-start | bytes 3145736 | tf_op jit(solution)/shard_map/ppermute | solution.py:145
  99.7 8.5 %collective-permute-start.8 = (bf16[512,256]{0,1:T(8,128)(2,1)S(1)}, bf16[512,256]{0,1:T(8,128)(2,1)}, u32[]{:S(2)}, u32[]{:S(2)}) collective-permute-start(bf16[512,256]{0,1:T(8,128)(2,1)S(1)} %constant_dynamic-slice_fusion.1), channel_id=1, source_target_pairs={{0,4},{4,0},{1,5},{5,1},{2,6},{6,2},{3,7},{7,3},{8,12},{12,8},{9,1... | collective-permute-start | bytes 786440 | tf_op jit(solution)/shard_map/ppermute | solution.py:163
  101.3 9.6 %collective-permute-start.6 = (bf16[1024,128]{0,1:T(8,128)(2,1)S(1)}, bf16[1024,128]{0,1:T(8,128)(2,1)S(1)}, u32[]{:S(2)}, u32[]{:S(2)}) collective-permute-start(bf16[1024,128]{0,1:T(8,128)(2,1)S(1)} %constant_dynamic-slice_fusion.3), channel_id=1, source_target_pairs={{0,16},{8,24},{16,0},{24,8},{1,17},{9,25},{17,1},{25,9},{2,18},{10... | collective-permute-start | bytes 786440 | tf_op jit(solution)/shard_map/ppermute | solution.py:145
  109.3 5.0 %collective-permute-start.9 = (bf16[512,128]{0,1:T(8,128)(2,1)S(1)}, bf16[512,128]{0,1:T(8,128)(2,1)S(1)}, u32[]{:S(2)}, u32[]{:S(2)}) collective-permute-start(bf16[512,128]{0,1:T(8,128)(2,1)S(1)} %constant_dynamic-slice_fusion), channel_id=1, source_target_pairs={{0,16},{8,24},{16,0},{24,8},{1,17},{9,25},{17,1},{25,9},{2,18},{10... | collective-permute-start | bytes 393224 | tf_op jit(solution)/shard_map/ppermute | solution.py:145
  111.0 5.0 %collective-permute-start.7 = (bf16[512,128]{0,1:T(8,128)(2,1)S(1)}, bf16[512,128]{0,1:T(8,128)(2,1)S(1)}, u32[]{:S(2)}, u32[]{:S(2)}) collective-permute-start(bf16[512,128]{0,1:T(8,128)(2,1)S(1)} %constant_dynamic-slice_fusion.2), channel_id=1, source_target_pairs={{0,4},{4,0},{1,5},{5,1},{2,6},{6,2},{3,7},{7,3},{8,12},{12,8},{9,1... | collective-permute-start | bytes 393224 | tf_op jit(solution)/shard_map/ppermute | solution.py:163
  116.1 6.2 %collective-permute-start.10 = (bf16[128,256]{0,1:T(8,128)(2,1)S(1)}, bf16[128,256]{0,1:T(8,128)(2,1)S(1)}, u32[]{:S(2)}, u32[]{:S(2)}) collective-permute-start(bf16[128,256]{0,1:T(8,128)(2,1)S(1)} %get-tuple-element.20), channel_id=1, source_target_pairs={{0,1},{1,2},{2,3},{3,0},{4,5},{5,6},{6,7},{7,4},{8,9},{9,10},{10,1... | collective-permute-start | bytes 196616 | tf_op jit(solution)/shard_map/ppermute | solution.py:163
  117.0 6.6 %collective-permute-start.11 = (bf16[128,256]{0,1:T(8,128)(2,1)S(1)}, bf16[128,256]{0,1:T(8,128)(2,1)S(1)}, u32[]{:S(2)}, u32[]{:S(2)}) collective-permute-start(bf16[128,256]{0,1:T(8,128)(2,1)S(1)} %get-tuple-element.21), channel_id=1, source_target_pairs={{0,2},{1,3},{2,0},{3,1},{4,6},{5,7},{6,4},{7,5},{8,10},{9,11},{10,... | collective-permute-start | bytes 196616 | tf_op jit(solution)/shard_map/ppermute | solution.py:163
  118.1 5.5 %collective-permute-start.12 = (bf16[128,256]{0,1:T(8,128)(2,1)S(1)}, bf16[128,256]{0,1:T(8,128)(2,1)S(1)}, u32[]{:S(2)}, u32[]{:S(2)}) collective-permute-start(bf16[128,256]{0,1:T(8,128)(2,1)S(1)} %get-tuple-element.22), channel_id=1, source_target_pairs={{0,3},{1,0},{2,1},{3,2},{4,7},{5,4},{6,5},{7,6},{8,11},{9,8},{10,9... | collective-permute-start | bytes 196616 | tf_op jit(solution)/shard_map/ppermute | solution.py:163
  123.6 6.3 %collective-permute-start.13 = (bf16[128,256]{0,1:T(8,128)(2,1)S(1)}, bf16[128,256]{0,1:T(8,128)(2,1)S(1)}, u32[]{:S(2)}, u32[]{:S(2)}) collective-permute-start(bf16[128,256]{0,1:T(8,128)(2,1)S(1)} %add_convert_fusion.6), channel_id=1, source_target_pairs={{0,8},{8,0},{16,24},{24,16},{1,9},{9,1},{17,25},{25,17},{2,10},{10... | collective-permute-start | bytes 196616 | tf_op jit(solution)/shard_map/ppermute | solution.py:145
  123.7 6.2 %collective-permute-start.14 = (bf16[128,256]{0,1:T(8,128)(2,1)S(1)}, bf16[128,256]{0,1:T(8,128)(2,1)S(1)}, u32[]{:S(2)}, u32[]{:S(2)}) collective-permute-start(bf16[128,256]{0,1:T(8,128)(2,1)S(1)} %add_convert_fusion.6), channel_id=1, source_target_pairs={{0,16},{8,24},{16,0},{24,8},{1,17},{9,25},{17,1},{25,9},{2,18},{10... | collective-permute-start | bytes 196616 | tf_op jit(solution)/shard_map/ppermute | solution.py:145
  124.2 5.7 %collective-permute-start.15 = (bf16[128,256]{0,1:T(8,128)(2,1)S(1)}, bf16[128,256]{0,1:T(8,128)(2,1)S(1)}, u32[]{:S(2)}, u32[]{:S(2)}) collective-permute-start(bf16[128,256]{0,1:T(8,128)(2,1)S(1)} %add_convert_fusion.6), channel_id=1, source_target_pairs={{0,24},{8,16},{16,8},{24,0},{1,25},{9,17},{17,9},{25,1},{2,26},{10... | collective-permute-start | bytes 196616 | tf_op jit(solution)/shard_map/ppermute | solution.py:145
where the time goes:
time: 132 us; the launch traced here: 131 us
  matrix products  37.3 us (28%)
  waiting for transfers between devices  29.4 us (22%)
  starting transfers between devices  24 us (18%)
  Pallas kernels  21.5 us (16%)
  other arithmetic  10.7 us (8%)
  local copies, waits for them, and re-layouts  7.15 us (5%)
    dot_general x6, matrix products, project(): jnp.dot(normalize(values, gain), weights, preferred_element_type=F32)  26.5 us
    pallas_call x2, Pallas kernels, spatial_attend(): pl.pallas_call(functools.partial(spatial_kernel, rows, cols, all_rows), g...  14.2 us
    ppermute x5, waiting for transfers between devices, scatter_rows(): arrived = lax.ppermute(take((me + shift) % n), axis, cyclic(axis, shift))  9.68 us
    ppermute x5, starting transfers between devices, scatter_rows(): arrived = lax.ppermute(take((me + shift) % n), axis, cyclic(axis, shift))  7.88 us
    ppermute x1, waiting for transfers between devices, per_device(): lax.ppermute(block, 'tm', cyclic('tm', shift))  7.59 us
    pallas_call x1, Pallas kernels, temporal_attend(): pl.pallas_call(functools.partial(temporal_kernel, frames, keys), grid=(to...  7.3 us
    ppermute x6, starting transfers between devices, exchange_bit(): return lax.ppermute(value, axis, [(i, i ^ bit) for i in range(n)])  5.17 us
    ppermute x1, waiting for transfers between devices, per_device(): lax.ppermute(here[:, :HALO], 'space', down).reshape(frames * span, depth)  4.89 us
  transfers between devices with their start and end apart: 16, of which 10 were waited for; matrix products, arithmetic and copies ran while one was open for 23% of the time, Pallas kernels for 5%

commit v1 on v0

v1 whole, which is shorter than its diff:
```python
import functools

import jax
import jax.numpy as jnp
from jax import lax
from jax.experimental import pallas as pl
from jax.experimental.pallas import tpu as pltpu
from jax.sharding import PartitionSpec as P

HALO = 4
HEADS = 16
HEAD_DIM = 64
LANES = 128
TILE = 512
SCALE = HEAD_DIM ** (-0.5)
FLOOR = 0.5
BF = jnp.bfloat16
F32 = jnp.float32
MESH = pl.DeviceIdType.MESH


def block_kernel(dims, *refs):
    ranks, places, parts, frames, chunks, pc, depth = dims
    (clip, order_ref, reach_ref, gain_one, gain_two, w_one, m_one, w_two, m_two, cot_in,
     out, grad,
     xx, pr, nb, w1, o1, w2, o2, ctx1, mid, mids, qs, ks, vs, ctx2, cot, gather, spread, bias, acc,
     axr, a1, ayr, byr, b1, bxr, zb, zr, gp, gr, outv,
     s_load, s_xs, s_xr, s_zs, s_zr, s_ms, s_mr, s_cs, s_cr, s_gs, s_gr, s_out) = refs
    blk = HALO * pc
    span = blk * ranks
    cols = pc * ranks
    tokens = chunks * span
    rows = chunks * HALO
    keys = ranks * frames
    half = depth // 2
    quarter = half // 2
    t, s, b = lax.axis_index("tm"), lax.axis_index("space"), lax.axis_index("batch")
    core, y = b % 2, b // 2
    ny = parts // 2
    lane_part = quarter // ny
    own_rows = depth // ranks
    piece_rows = own_rows // places

    loads = {}

    def load(name, src, dst):
        copy = pltpu.make_async_copy(src, dst, s_load.at[len(loads)])
        copy.start()
        loads[name] = copy

    def ready(*names):
        for name in names:
            loads[name].wait()

    for f in range(frames):
        load(f"x{f}", clip.at[t * frames + f], xx.at[f, 1:chunks + 1, t])
    for part in range(3):
        load(f"w1{part}", w_one.at[:, part * depth:(part + 1) * depth], w1.at[:, part * depth:(part + 1) * depth])
    load("o1", m_one, o1)
    load("w2", w_two, w2)
    load("o2", m_two, o2)
    load("cot", cot_in.at[:, pl.ds(pl.multiple_of(core * half, half), half)], cot.at[0])

    barrier = pltpu.get_barrier_semaphore()
    for axis, me, count in (("tm", t, ranks), ("space", s, places), ("batch", b, parts)):
        for shift in range(1, count):
            pl.semaphore_signal(barrier, inc=1, device_id={axis: (me + shift) % count}, device_id_type=MESH)
    pl.semaphore_wait(barrier, ranks + places + parts - 3)

    def remote(src, dst, send, recv, axis, to):
        return pltpu.make_async_remote_copy(src, dst, send, recv, device_id={axis: to}, device_id_type=MESH)

    x_copies = {}
    for f in range(frames):
        for j in range(1, ranks):
            to = (t + j) % ranks
            copy = remote(clip.at[to * frames + f], xx.at[f, 1:chunks + 1, t], s_xs.at[f, j - 1], s_xr.at[f, j - 1],
                          "tm", to)
            copy.start()
            x_copies[f, j] = copy

    def halo(f, j, up):
        source = (t - j) % ranks
        slot, dest = (1, chunks + 1) if up else (chunks, 0)
        src = xx.at[f, slot, source]
        if j == 0:
            src = clip.at[t * frames + f, slot - 1]
        return remote(src, xx.at[f, dest, source], s_zs.at[int(up), f, j], s_zr.at[int(up), f, j],
                      "space", (s - 1) if up else (s + 1))

    def send_halo(f, j):
        @pl.when(s > 0)
        def _():
            halo(f, j, True).start()

        @pl.when(s < places - 1)
        def _():
            halo(f, j, False).start()

    def wait_halo(f, j):
        @pl.when(s > 0)
        def _():
            halo(f, j, False).wait_recv()

        @pl.when(s < places - 1)
        def _():
            halo(f, j, True).wait_recv()

    def finish_halo(f, j):
        @pl.when(s > 0)
        def _():
            halo(f, j, True).wait_send()

        @pl.when(s < places - 1)
        def _():
            halo(f, j, False).wait_send()

    for f in range(frames):
        send_halo(f, 0)
    other_core = b + 1 - 2 * core
    cot_copy = remote(cot_in.at[:, pl.ds(pl.multiple_of((1 - core) * half, half), half)], cot.at[1],
                      s_cs.at[0], s_cr.at[0], "batch", other_core)
    cot_copy.start()

    @pl.when(s == 0)
    def _():
        xx[:, 0] = jnp.zeros((frames, ranks, blk, depth), BF)

    @pl.when(s == places - 1)
    def _():
        xx[:, chunks + 1] = jnp.zeros((frames, ranks, blk, depth), BF)

    lane = lax.broadcasted_iota(jnp.int32, (1, LANES), 1)
    first_head = (lane < HEAD_DIM).astype(F32)
    masks = (first_head.astype(BF), (1.0 - first_head).astype(BF))
    head = lax.broadcasted_iota(jnp.int32, (depth, LANES), 0) // HEAD_DIM
    gather[...] = (head == lax.broadcasted_iota(jnp.int32, (depth, LANES), 1)).astype(F32).astype(BF)
    head = lax.broadcasted_iota(jnp.int32, (LANES, depth), 1) // HEAD_DIM
    spread[...] = (head == lax.broadcasted_iota(jnp.int32, (LANES, depth), 0)).astype(F32).astype(BF)
    for f in range(frames):
        for chunk in range(chunks):
            shape = (span, 3 * span)
            q_row = chunk * HALO + lax.broadcasted_iota(jnp.int32, shape, 0) % blk // pc
            k_at = lax.broadcasted_iota(jnp.int32, shape, 1)
            k_row = (chunk - 1 + k_at // span) * HALO + k_at % blk // pc
            place = s * rows + k_row
            kept = (jnp.abs(k_row - q_row) <= reach_ref[f]) & (place >= 0) & (place < rows * places)
            bias[f, chunk] = jnp.where(kept, 0.0, -1e30)

    def normalize(values, gain):
        widened = values.astype(F32)
        scaled = widened * lax.rsqrt(jnp.mean(widened * widened, axis=-1, keepdims=True) + FLOOR)
        return (scaled * gain[...]).astype(BF)

    def project_spatial(blocks, first):
        for i, (f, slot, source) in enumerate(blocks):
            nb[i * blk:(i + 1) * blk] = normalize(xx[f, slot, source], gain_one)
        count = len(blocks) * blk
        per = depth // TILE

        def step(i, carry):
            at = pl.ds(pl.multiple_of(i * TILE, TILE), TILE)
            lanes = pl.ds(pl.multiple_of(i % per * TILE, TILE), TILE)
            got = jnp.dot(nb[:count], w1[:, at], preferred_element_type=F32).astype(BF)
            for k, (f, slot, source) in enumerate(blocks):
                pr[i // per, f, slot, source, :, lanes] = got[k * blk:(k + 1) * blk]
            return carry

        lax.fori_loop(first * per, 3 * per, step, 0)

    own = range(1, chunks + 1)
    ends = (0, chunks + 1)
    ready(*[f"x{f}" for f in range(frames)], "w10", "w11", "w12")
    project_spatial([(f, slot, t) for f in range(frames) for slot in own], 0)
    for f in range(frames):
        wait_halo(f, 0)
    project_spatial([(f, slot, t) for f in range(frames) for slot in ends], 1)
    for f in range(frames):
        for j in range(1, ranks):
            x_copies[f, j].wait_recv()
            send_halo(f, j)
        project_spatial([(f, slot, (t - j) % ranks) for j in range(1, ranks) for slot in own], 0)

    def attend_spatial(f):
        ones = jnp.ones((3 * span, LANES), BF)

        def pair_step(pair, carry):
            at = pl.ds(pl.multiple_of(pair * LANES, LANES), LANES)
            for chunk in range(chunks):
                q = pr[0, f, 1 + chunk, :, :, at].reshape(span, LANES) * BF(SCALE)
                both = jnp.concatenate([q * masks[0], q * masks[1]], axis=0)
                k = pr[1, f, chunk:chunk + 3, :, :, at].reshape(3 * span, LANES)
                v = pr[2, f, chunk:chunk + 3, :, :, at].reshape(3 * span, LANES)
                sc = lax.dot_general(both, k, (((1,), (1,)), ((), ())), preferred_element_type=F32)
                sc = sc + jnp.concatenate([bias[f, chunk], bias[f, chunk]], axis=0)
                p = jnp.exp(sc - jnp.max(sc, axis=-1, keepdims=True)).astype(BF)
                o = jnp.dot(p, jnp.concatenate([v, ones], axis=1), preferred_element_type=F32)
                o = o[:, :LANES] / o[:, LANES:]
                ctx1[chunk * span:(chunk + 1) * span, at] = jnp.where(lane < HEAD_DIM, o[:span], o[span:]).astype(BF)
            return carry

        lax.fori_loop(0, depth // LANES, pair_step, 0)

    def merge_spatial(f):
        def step(i, carry):
            at = pl.ds(pl.multiple_of(i * TILE, TILE), TILE)
            got = jnp.dot(ctx1[...], o1[:, at], preferred_element_type=F32)
            for chunk in range(chunks):
                for source in range(ranks):
                    base = chunk * span + source * blk
                    total = (got[base:base + blk] + xx[f, 1 + chunk, source, :, at].astype(F32)).astype(BF)
                    for r in range(HALO):
                        row = (chunk * HALO + r) * cols + source * pc
                        mid[f, row:row + pc, at] = total[r * pc:(r + 1) * pc]
            return carry

        lax.fori_loop(0, depth // TILE, step, 0)

    ready("o1")
    m_copies = {}
    for f in range(frames):
        for j in range(1, ranks):
            wait_halo(f, j)
        project_spatial([(f, slot, (t - j) % ranks) for j in range(1, ranks) for slot in ends], 1)
        attend_spatial(f)
        merge_spatial(f)
        for j in range(1, ranks):
            copy = remote(mid.at[f], mids.at[j - 1, f], s_ms.at[f, j - 1], s_mr.at[f, j - 1], "tm", (t + j) % ranks)
            copy.start()
            m_copies[f, j] = copy

    def project_temporal(read, key, query):
        for i in range(0, tokens, 64):
            nb[i:i + 64] = normalize(read(i, 64), gain_two)
        per = depth // TILE

        def make(dst, part):
            def step(i, carry):
                at = pl.ds(pl.multiple_of(part * depth + i * TILE, TILE), TILE)
                lanes = pl.ds(pl.multiple_of(i * TILE, TILE), TILE)
                dst[:, lanes] = jnp.dot(nb[:tokens], w2[:, at], preferred_element_type=F32).astype(BF)
                return carry
            return step

        if query is not None:
            lax.fori_loop(0, per, make(qs.at[query], 0), 0)
        lax.fori_loop(0, per, make(ks.at[key], 1), 0)
        lax.fori_loop(0, per, make(vs.at[key], 2), 0)

    ready("w2")
    for f in range(frames):
        project_temporal(lambda i, n, f=f: mid[f, i:i + n], f, f)
    for f in range(frames):
        for j in range(1, ranks):
            m_copies[f, j].wait_recv()
            project_temporal(lambda i, n, f=f, j=j: mids[j - 1, f, i:i + n], j * frames + f, None)

    k_order = [order_ref[(t - j) % ranks * frames + g] for j in range(ranks) for g in range(frames)]
    size = 32

    def attend_temporal(f):
        def step(i, carry):
            at = pl.ds(pl.multiple_of(i * size, size), size)
            q = qs[f, at] * BF(SCALE)
            scores = []
            for g in range(keys):
                sc = jnp.dot(q * ks[g, at], gather[...], preferred_element_type=F32)
                scores.append(sc + jnp.where(k_order[g] <= k_order[f], 0.0, -1e30))
            top_score = functools.reduce(jnp.maximum, scores)
            exps = [jnp.exp(sc - top_score) for sc in scores]
            scale = 1.0 / functools.reduce(jnp.add, exps)
            total = None
            for g in range(keys):
                w = jnp.dot((exps[g] * scale).astype(BF), spread[...], preferred_element_type=F32)
                term = w * vs[g, at].astype(F32)
                total = term if total is None else total + term
            ctx2[0, pl.ds(pl.multiple_of(f * tokens + i * size, size), size)] = total.astype(BF)
            return carry

        lax.fori_loop(0, tokens // size, step, 0)

    c_copies = []
    for f in range(frames):
        attend_temporal(f)
        at = slice(f * tokens, (f + 1) * tokens)
        copy = remote(ctx2.at[0, at], ctx2.at[1, at], s_cs.at[1 + f], s_cr.at[1 + f], "batch", other_core)
        copy.start()
        c_copies.append(copy)

    ready("cot", "o2")
    cot_copy.wait()
    for copy in c_copies:
        copy.wait()
    row_tile = 256

    def grad_step(i, carry):
        at = pl.ds(pl.multiple_of(i * row_tile, row_tile), row_tile)
        total = None
        for which in range(2):
            got = lax.dot_general(ctx2[which, :, at], cot[which], (((0,), (0,)), ((), ())),
                                  preferred_element_type=F32)
            total = got if total is None else total + got
        acc[at] = total.astype(BF)
        return carry

    lax.fori_loop(0, depth // row_tile, grad_step, 0)

    sems = iter(range(s_gs.shape[0]))

    def exchange(axis, me, count, pieces, dests, slots=None):
        copies = []
        for k in range(1, count):
            to = (me + k) % count
            n = next(sems)
            copy = remote(pieces(to), dests.at[k - 1], s_gs.at[n], s_gr.at[n], axis, to)
            copy.start()
            copies.append(copy)
        return copies

    def over_y(pieces, dests):
        copies = []
        for k in range(1, ny):
            to = (y + k) % ny
            n = next(sems)
            copy = remote(pieces(to), dests.at[k - 1], s_gs.at[n], s_gr.at[n], "batch", to * 2 + core)
            copy.start()
            copies.append(copy)
        return copies

    def wait(copies):
        for copy in copies:
            copy.wait()

    def rows_of(to):
        return pl.ds(pl.multiple_of(to * own_rows, own_rows), own_rows)

    def lanes_of(base, to):
        return pl.ds(pl.multiple_of(base + to * lane_part, lane_part), lane_part)

    one_x = exchange("tm", t, ranks, lambda to: acc.at[rows_of(to), 0:quarter], axr)
    two_y = over_y(lambda to: acc.at[:, lanes_of(quarter, to)], byr)

    for f in range(frames):
        def out_step(i, carry, f=f):
            at = pl.ds(pl.multiple_of(i * TILE, TILE), TILE)
            got = jnp.dot(ctx2[0, f * tokens:(f + 1) * tokens], o2[:, at], preferred_element_type=F32)
            outv[f, :, at] = (mid[f, :, at].astype(F32) + got).astype(BF)
            return carry

        lax.fori_loop(0, depth // TILE, out_step, 0)
    out_copy = pltpu.make_async_copy(outv, out, s_out)
    out_copy.start()

    def total_of(first, received, count):
        total = first.astype(F32)
        for k in range(count - 1):
            total = total + received[k].astype(F32)
        return total

    wait(one_x)
    a1[...] = total_of(acc[rows_of(t), 0:quarter], axr, ranks).astype(BF)
    one_y = over_y(lambda to: a1.at[:, lanes_of(0, to)], ayr)
    wait(two_y)
    b1[...] = total_of(acc[:, lanes_of(quarter, y)], byr, ny).astype(BF)
    two_x = exchange("tm", t, ranks, lambda to: b1.at[rows_of(to)], bxr)
    wait(one_y)
    zb[:, :lane_part] = total_of(a1[:, lanes_of(0, y)], ayr, ny).astype(BF)
    wait(two_x)
    zb[:, lane_part:] = total_of(b1[rows_of(t)], bxr, ranks).astype(BF)

    def block_of(to):
        return pl.ds(pl.multiple_of(to * piece_rows, piece_rows), piece_rows)

    wait(exchange("space", s, places, lambda to: zb.at[block_of(to)], zr))
    gp[...] = total_of(zb[block_of(s)], zr, places).astype(BF)
    last = exchange("batch", b, parts, lambda to: gp, gr)

    def place_piece(owner, value):
        base = owner % 2 * half + owner // 2 * lane_part
        grad[:, pl.ds(pl.multiple_of(base, lane_part), lane_part)] = value[:, :lane_part].astype(F32)
        grad[:, pl.ds(pl.multiple_of(base + quarter, lane_part), lane_part)] = value[:, lane_part:].astype(F32)

    place_piece(b, gp[...])
    for k, copy in enumerate(last):
        copy.wait()
        place_piece((b - 1 - k) % parts, gr[k])

    for copy in x_copies.values():
        copy.wait_send()
    for copy in m_copies.values():
        copy.wait_send()
    for f in range(frames):
        for j in range(ranks):
            finish_halo(f, j)
    out_copy.wait()


def per_device(clip_tokens, frame_order, row_reach, spatial_gain, spatial_heads, spatial_merge,
               temporal_gain, temporal_heads, temporal_merge, cotangent):
    ranks, places, parts = lax.axis_size("tm"), lax.axis_size("space"), lax.axis_size("batch")
    _, all_frames, rows, pc, depth = clip_tokens.shape
    frames, cols = all_frames // ranks, pc * ranks
    chunks, blk, tokens = rows // HALO, HALO * pc, rows * cols
    span = blk * ranks
    keys = ranks * frames
    ny = parts // 2
    half, quarter = depth // 2, depth // 4
    lane_part, own_rows = quarter // ny, depth // ranks
    piece_rows = own_rows // places
    dims = (ranks, places, parts, frames, chunks, pc, depth)
    anywhere = pl.BlockSpec(memory_space=pl.ANY)
    smem = pl.BlockSpec(memory_space=pltpu.SMEM)
    vmem = pl.BlockSpec(memory_space=pltpu.VMEM)
    dma = pltpu.SemaphoreType.DMA
    others = max(ranks - 1, 1)
    most = max(2 * frames * chunks, 2 * frames * 2, (ranks - 1) * max(chunks, 2)) * blk
    steps = 2 * (ranks - 1) + 2 * (ny - 1) + (places - 1) + (parts - 1)
    scratch = [
        pltpu.VMEM((frames, chunks + 2, ranks, blk, depth), BF),
        pltpu.VMEM((3, frames, chunks + 2, ranks, blk, depth), BF),
        pltpu.VMEM((max(most, tokens), depth), BF),
        pltpu.VMEM((depth, 3 * depth), BF),
        pltpu.VMEM((depth, depth), BF),
        pltpu.VMEM((depth, 3 * depth), BF),
        pltpu.VMEM((depth, depth), BF),
        pltpu.VMEM((tokens, depth), BF),
        pltpu.VMEM((frames, tokens, depth), BF),
        pltpu.VMEM((others, frames, tokens, depth), BF),
        pltpu.VMEM((frames, tokens, depth), BF),
        pltpu.VMEM((keys, tokens, depth), BF),
        pltpu.VMEM((keys, tokens, depth), BF),
        pltpu.VMEM((2, frames * tokens, depth), BF),
        pltpu.VMEM((2, frames * tokens, half), BF),
        pltpu.VMEM((depth, LANES), BF),
        pltpu.VMEM((LANES, depth), BF),
        pltpu.VMEM((frames, chunks, span, 3 * span), F32),
        pltpu.VMEM((depth, half), BF),
        pltpu.VMEM((others, own_rows, quarter), BF),
        pltpu.VMEM((own_rows, quarter), BF),
        pltpu.VMEM((max(ny - 1, 1), own_rows, lane_part), BF),
        pltpu.VMEM((max(ny - 1, 1), depth, lane_part), BF),
        pltpu.VMEM((depth, lane_part), BF),
        pltpu.VMEM((others, own_rows, lane_part), BF),
        pltpu.VMEM((own_rows, 2 * lane_part), BF),
        pltpu.VMEM((max(places - 1, 1), piece_rows, 2 * lane_part), BF),
        pltpu.VMEM((piece_rows, 2 * lane_part), BF),
        pltpu.VMEM((parts - 1, piece_rows, 2 * lane_part), BF),
        pltpu.VMEM((frames, tokens, depth), BF),
        dma((frames + 7,)),
        dma((frames, others)), dma((frames, others)),
        dma((2, frames, ranks)), dma((2, frames, ranks)),
        dma((frames, others)), dma((frames, others)),
        dma((1 + frames,)), dma((1 + frames,)),
        dma((steps,)), dma((steps,)),
        dma,
    ]
    out, grad = pl.pallas_call(
        functools.partial(block_kernel, dims),
        out_shape=(jax.ShapeDtypeStruct((frames, tokens, depth), BF),
                   jax.ShapeDtypeStruct((piece_rows, depth), F32)),
        in_specs=[anywhere, smem, smem, vmem, vmem] + [anywhere] * 5,
        out_specs=(anywhere, vmem),
        scratch_shapes=scratch,
        compiler_params=pltpu.CompilerParams(collective_id=0, has_side_effects=True,
                                             vmem_limit_bytes=67043328),
        name="block",
    )(clip_tokens.reshape(all_frames, chunks, blk, depth), frame_order.reshape(-1), row_reach.reshape(-1),
      spatial_gain.reshape(1, depth), temporal_gain.reshape(1, depth),
      spatial_heads, spatial_merge, temporal_heads, temporal_merge, cotangent.reshape(-1, depth))
    return out.reshape(1, frames, rows, cols, depth), grad


def solution(mesh):
    in_specs = (
        P("batch", None, "space", "tm", None),
        P("batch", None),
        P("batch", "tm"),
        P(),
        P(),
        P(),
        P(),
        P(),
        P(),
        P("batch", "tm", "space", None, None),
    )
    out_specs = (P("batch", "tm", "space", None, None), P(("tm", "space"), None))
    return jax.shard_map(per_device, mesh=mesh, in_specs=in_specs, out_specs=out_specs, check_vma=False)
```

time: 132 us -> 95 us (0.72)
  Pallas kernels: 21.5 us -> 89.9 us
  matrix products: 37.3 us -> 0 us
  waiting for transfers between devices: 29.4 us -> 0 us
  starting transfers between devices: 24 us -> 0 us
  other arithmetic: 10.7 us -> 0 us
  local copies, waits for them, and re-layouts: 7.15 us -> 4.17 us
    pallas_call x3 -> x1, Pallas kernels: 21.5 us -> 89.9 us  [per_device(): pl.pallas_call(functools.partial(block_kernel, dims), out_shape=(jax.Shap...]
    dot_general x10 -> x0, matrix products: 37.3 us -> none  [the longest x6 26.5 us: project(): jnp.dot(normalize(values, gain), weights, preferred_element_type=F32)]
    ppermute x16 -> x0, waiting for transfers between devices: 29.4 us -> none  [the longest x5 9.68 us: scatter_rows(): arrived = lax.ppermute(take((me + shift) % n), axis, cyclic(axis, shift))]
    ppermute x16 -> x0, starting transfers between devices: 24 us -> none  [the longest x5 7.88 us: scatter_rows(): arrived = lax.ppermute(take((me + shift) % n), axis, cyclic(axis, shift))]
    convert_element_type x9 -> x0, other arithmetic: 5.1 us -> none  [the longest x3 2.04 us: halve_columns(): return (kept.astype(F32) + arrived.astype(F32)).astype(BF)]
    slice x3 -> x0, local copies, waits for them, and re-layouts: 2.47 us -> none  [the longest x1 1.34 us: per_device(): reach_now = reach[f:f + 1]]
    another operation x3 -> x0, other arithmetic: 2.46 us -> none  [per_device(): jnp.stack([lax.select_n((me - j) % ranks, *pieces) if ranks > 2 else jnp....]
    reduce_sum x5 -> x0, other arithmetic: 2.31 us -> none  [normalize(): jnp.mean(widened * widened, axis=-1, keepdims=True) + FLOOR]
  transfers between devices with their start and end apart: 16 -> 0, of which waited for: 10 -> 0; matrix products, arithmetic and copies ran while one was open for 23% -> 0% of each run, Pallas kernels for 5% -> 0%
where the time goes in v1:
time: 95 us; the launch traced here: 94.7 us
  Pallas kernels  89.9 us (95%)
  local copies, waits for them, and re-layouts  4.17 us (4%)
    pallas_call x1, Pallas kernels, per_device(): pl.pallas_call(functools.partial(block_kernel, dims), out_shape=(jax.Shap...  89.9 us
    unnamed x2, local copies, waits for them, and re-layouts  4.17 us

profile of v1, /device:TPU:0, one launch (start us, length us, event | category | flops | bytes accessed | tf_op | source)
XLA Modules:
  0.0 94.7 jit_solution(11069603950909881417)
XLA Ops:
  0.6 89.9 %block.1 = (bf16[2,256,1024]{2,1,0:T(8,128)(2,1)}, f32[128,1024]{1,0:T(8,128)}) custom-call(bf16[4,2,64,1024]{3,2,1,0:T(8,128)(2,1)} %bitcast.7, s32[4]{0:T(128)} %bitcast.12, s32[2]{0:T(128)} %bitcast.13, f32[1,1024]{1,0:T(1,128)} %bitcast.10, f32[1,1024]{1,0:T(1,128)} %bitcast.11, bf16[1024,3072]{1,0:T(8,128)(2,1)} %refs_5_.1, bf16[1024,1024]{1,0:T(8,128)(2,1)} %refs_6_.1, ...), custom_call_target="tpu_custom_call" | custom-call | tf_op jit(solution)/shard_map/block/pallas_call | solution.py:457
  90.5 2.3 %copy.14 = bf16[1,2,8,32,1024]{4,3,2,1,0:T(8,128)(2,1)} copy(bf16[1,2,8,32,1024]{4,3,2,1,0:T(8,128)(2,1)} %bitcast.9) | data formatting | bytes 2097152
  92.8 1.9 %copy.15 = f32[128,1024]{1,0:T(8,128)} copy(f32[128,1024]{1,0:T(8,128)} %get-tuple-element.9) | data formatting | bytes 1048576

commit v2 on v1

v2 whole, which is shorter than its diff:
```python
import functools

import jax
import jax.numpy as jnp
from jax import lax
from jax.experimental import pallas as pl
from jax.experimental.pallas import tpu as pltpu
from jax.sharding import PartitionSpec as P

HALO = 4
HEADS = 16
HEAD_DIM = 64
LANES = 128
TILE = 1024
PIECE = 64
UNROLL = 8
SCALE = HEAD_DIM ** (-0.5)
FLOOR = 0.5
BF = jnp.bfloat16
F32 = jnp.float32
MESH = pl.DeviceIdType.MESH


def block_kernel(dims, *refs):
    ranks, places, parts, frames, chunks, pc, depth = dims
    (clip, order_ref, reach_ref, gain_one, gain_two, w_one, m_one, w_two, m_two, cot_in,
     out, grad,
     xx, away_x, pr, nb, w1, o1, w2, o2, ctx1, mid, mids, qs, ks, vs, ctx2, cot, gather, spread, bias, accf, acc,
     xr_one, yr_one, one_x, one_y, xr_two, yr_two, two, zr, gp, gr,
     s_load, s_xs, s_xr, s_zs, s_zr, s_ms, s_mr, s_cs, s_cr, s_gs, s_gr, s_out) = refs
    blk = HALO * pc
    span = blk * ranks
    cols = pc * ranks
    tokens = chunks * span
    rows = chunks * HALO
    keys = ranks * frames
    half = depth // 2
    t, s, b = lax.axis_index("tm"), lax.axis_index("space"), lax.axis_index("batch")
    core, y = b % 2, b // 2
    ny = parts // 2

    loads = {}

    def load(name, src, dst):
        copy = pltpu.make_async_copy(src, dst, s_load.at[len(loads)])
        copy.start()
        loads[name] = copy

    def ready(*names):
        for name in names:
            loads[name].wait()

    def half_of(which):
        return pl.ds(pl.multiple_of(which * half, half), half)

    for f in range(frames):
        load(f"x{f}", clip.at[t * frames + f], xx.at[f, 1:chunks + 1, t])
        for j in range(1, ranks):
            load(f"y{f}{j}", clip.at[(t + j) % ranks * frames + f], away_x.at[j - 1, f])
    for part in range(3):
        load(f"w1{part}", w_one.at[:, part * depth:(part + 1) * depth], w1.at[:, part * depth:(part + 1) * depth])
    load("o1", m_one, o1)
    load("w2", w_two, w2)
    load("o2", m_two, o2)
    for f in range(frames):
        load(f"cot{f}", cot_in.at[f, :, :, half_of(core)], cot.at[0, :, f])

    barrier = pltpu.get_barrier_semaphore()
    for axis, me, count in (("tm", t, ranks), ("space", s, places), ("batch", b, parts)):
        for shift in range(1, count):
            pl.semaphore_signal(barrier, inc=1, device_id={axis: (me + shift) % count}, device_id_type=MESH)
    pl.semaphore_wait(barrier, ranks + places + parts - 3)

    ready(*[f"x{f}" for f in range(frames)], *[f"y{f}{j}" for f in range(frames) for j in range(1, ranks)])
    def remote(src, dst, send, recv, axis, to):
        return pltpu.make_async_remote_copy(src, dst, send, recv, device_id={axis: to}, device_id_type=MESH)

    x_copies = {}
    for f in range(frames):
        for chunk in range(chunks):
            for j in range(1, ranks):
                to = (t + j) % ranks
                copy = remote(away_x.at[j - 1, f, chunk], xx.at[f, 1 + chunk, t],
                              s_xs.at[f, chunk, j - 1], s_xr.at[f, chunk, j - 1], "tm", to)
                copy.start()
                x_copies[f, chunk, j] = copy

    def halo(f, j, up):
        source = (t - j) % ranks
        slot, dest = (1, chunks + 1) if up else (chunks, 0)
        return remote(xx.at[f, slot, source], xx.at[f, dest, source], s_zs.at[int(up), f, j], s_zr.at[int(up), f, j],
                      "space", (s - 1) if up else (s + 1))

    def send_halo(f, j, up):
        @pl.when((s > 0) if up else (s < places - 1))
        def _():
            halo(f, j, up).start()

    def wait_halo(f, j, sides=(False, True)):
        for up in sides:
            @pl.when((s < places - 1) if up else (s > 0))
            def _():
                halo(f, j, up).wait_recv()

    def finish_halo(f, j):
        @pl.when(s > 0)
        def _():
            halo(f, j, True).wait_send()

        @pl.when(s < places - 1)
        def _():
            halo(f, j, False).wait_send()

    def forward(f, chunk):
        for j in range(1, ranks):
            x_copies[f, chunk, j].wait_recv()
            if chunk == 0:
                send_halo(f, j, True)
            if chunk == chunks - 1:
                send_halo(f, j, False)
        if f + 1 < frames and chunk == 0:
            send_halo(f + 1, 0, True)
        if f + 1 < frames and chunk == chunks - 1:
            send_halo(f + 1, 0, False)

    send_halo(0, 0, True)
    send_halo(0, 0, False)
    other_core = b + 1 - 2 * core
    cot_copies = []
    for f in range(frames):
        copy = remote(cot_in.at[f, :, :, half_of(1 - core)], cot.at[1, :, f], s_cs.at[f], s_cr.at[f],
                      "batch", other_core)
        copy.start()
        cot_copies.append(copy)

    @pl.when(s == 0)
    def _():
        xx[:, 0] = jnp.zeros((frames, ranks, blk, depth), BF)

    @pl.when(s == places - 1)
    def _():
        xx[:, chunks + 1] = jnp.zeros((frames, ranks, blk, depth), BF)

    lane = lax.broadcasted_iota(jnp.int32, (1, LANES), 1)
    first_head = (lane < HEAD_DIM).astype(F32)
    masks = (first_head.astype(BF), (1.0 - first_head).astype(BF))
    for f in range(frames):
        for chunk in range(chunks):
            shape = (span, 3 * span)
            q_row = chunk * HALO + lax.broadcasted_iota(jnp.int32, shape, 0) % blk // pc
            k_at = lax.broadcasted_iota(jnp.int32, shape, 1)
            k_row = (chunk - 1 + k_at // span) * HALO + k_at % blk // pc
            place = s * rows + k_row
            kept = (jnp.abs(k_row - q_row) <= reach_ref[f]) & (place >= 0) & (place < rows * places)
            bias[f, chunk] = jnp.where(kept, 0.0, -1e30)

    def normalize(values, gain):
        widened = values.astype(F32)
        scaled = widened * lax.rsqrt(jnp.mean(widened * widened, axis=-1, keepdims=True) + FLOOR)
        return (scaled * gain[...]).astype(BF)

    def project_spatial(blocks, first):
        for i, (f, slot, source) in enumerate(blocks):
            nb[i * blk:(i + 1) * blk] = normalize(xx[f, slot, source], gain_one)
        count = len(blocks) * blk
        per = depth // TILE

        def step(i, carry):
            at = pl.ds(pl.multiple_of(i * TILE, TILE), TILE)
            lanes = pl.ds(pl.multiple_of(i % per * TILE, TILE), TILE)
            got = jnp.dot(nb[:count], w1[:, at], preferred_element_type=F32).astype(BF)
            for k, (f, slot, source) in enumerate(blocks):
                pr[i // per, f, slot, source, :, lanes] = got[k * blk:(k + 1) * blk]
            return carry

        lax.fori_loop(first * per, 3 * per, step, 0)

    own = range(1, chunks + 1)
    ends = (0, chunks + 1)
    away = range(1, ranks)

    def attend_spatial(f, chunk):
        ones = jnp.ones((3 * span, LANES), BF)

        def pair_step(i, carry):
            for u in range(UNROLL):
                at = pl.ds(pl.multiple_of((UNROLL * i + u) * LANES, LANES), LANES)
                q = pr[0, f, 1 + chunk, :, :, at].reshape(span, LANES) * BF(SCALE)
                both = jnp.concatenate([q * masks[0], q * masks[1]], axis=0)
                k = pr[1, f, chunk:chunk + 3, :, :, at].reshape(3 * span, LANES)
                v = pr[2, f, chunk:chunk + 3, :, :, at].reshape(3 * span, LANES)
                sc = lax.dot_general(both, k, (((1,), (1,)), ((), ())), preferred_element_type=F32)
                sc = sc + jnp.concatenate([bias[f, chunk], bias[f, chunk]], axis=0)
                p = jnp.exp(sc - jnp.max(sc, axis=-1, keepdims=True)).astype(BF)
                o = jnp.dot(p, jnp.concatenate([v, ones], axis=1), preferred_element_type=F32)
                o = jnp.where(jnp.concatenate([lane, lane], axis=1) % LANES < HEAD_DIM, o[:span], o[span:])
                ctx1[:, at] = (o[:, :LANES] / o[:, LANES:]).astype(BF)
            return carry

        lax.fori_loop(0, depth // LANES // UNROLL, pair_step, 0)

    m_copies = {}

    def merge_spatial(f, chunk):
        def step(i, carry):
            at = pl.ds(pl.multiple_of(i * TILE, TILE), TILE)
            got = jnp.dot(ctx1[...], o1[:, at], preferred_element_type=F32)
            for source in range(ranks):
                base = source * blk
                total = (got[base:base + blk] + xx[f, 1 + chunk, source, :, at].astype(F32)).astype(BF)
                for r in range(HALO):
                    row = (chunk * HALO + r) * cols + source * pc
                    mid[f, row:row + pc, at] = total[r * pc:(r + 1) * pc]
            return carry

        lax.fori_loop(0, depth // TILE, step, 0)
        for piece in range(chunk * span // PIECE, (chunk + 1) * span // PIECE):
            at = slice(piece * PIECE, (piece + 1) * PIECE)
            for j in away:
                copy = remote(mid.at[f, at], mids.at[j - 1, f, at], s_ms.at[f, piece, j - 1],
                              s_mr.at[f, piece, j - 1], "tm", (t + j) % ranks)
                copy.start()
                m_copies[f, piece, j] = copy

    ready("w10", "w11", "w12")
    project_spatial([(f, slot, t) for f in range(frames) for slot in own], 0)
    for chunk in range(chunks - 1):
        forward(0, chunk)
    wait_halo(0, 0)
    project_spatial([(0, slot, t) for slot in ends], 1)
    forward(0, chunks - 1)
    project_spatial([(0, slot, (t - j) % ranks) for j in away for slot in own], 0)
    ready("o1")
    for f in range(frames):
        if f == 0:
            for j in away:
                wait_halo(f, j, (True,))
            project_spatial([(f, chunks + 1, (t - j) % ranks) for j in away], 1)
        else:
            for j in range(ranks):
                wait_halo(f, j)
            project_spatial([(f, slot, (t - j) % ranks) for j in range(ranks) for slot in ends], 1)
        if f + 1 < frames:
            for chunk in range(chunks - 1):
                forward(f + 1, chunk)
        for chunk in reversed(range(chunks)):
            if f == 0 and chunk == 0:
                for j in away:
                    wait_halo(f, j, (False,))
                project_spatial([(f, 0, (t - j) % ranks) for j in away], 1)
            attend_spatial(f, chunk)
            merge_spatial(f, chunk)
            if f + 1 < frames and chunk == chunks - 1:
                forward(f + 1, chunks - 1)
        if f + 1 < frames:
            project_spatial([(f + 1, slot, (t - j) % ranks) for j in away for slot in own], 0)

    head = lax.broadcasted_iota(jnp.int32, (depth, LANES), 0) // HEAD_DIM
    gather[...] = (head == lax.broadcasted_iota(jnp.int32, (depth, LANES), 1)).astype(F32).astype(BF)
    head = lax.broadcasted_iota(jnp.int32, (LANES, depth), 1) // HEAD_DIM
    spread[...] = (head == lax.broadcasted_iota(jnp.int32, (LANES, depth), 0)).astype(F32).astype(BF)

    def project_temporal(sources, parts_of, count):
        for i, read in enumerate(sources):
            nb[i * PIECE:(i + 1) * PIECE] = normalize(read(), gain_two)
        per = depth // TILE

        def make(dst, part):
            def step(i, carry):
                at = pl.ds(pl.multiple_of(part * depth + i * TILE, TILE), TILE)
                lanes = pl.ds(pl.multiple_of(i * TILE, TILE), TILE)
                got = jnp.dot(nb[:len(sources) * PIECE], w2[:, at], preferred_element_type=F32).astype(BF)
                for k, ref in enumerate(dst):
                    ref[:, lanes] = got[k * count:(k + 1) * count]
                return carry
            return step

        for part, dst in parts_of:
            lax.fori_loop(0, per, make(dst, part), 0)

    pieces = tokens // PIECE
    spot = lambda piece: slice(piece * PIECE, (piece + 1) * PIECE)
    ready("w2")
    for f in range(frames):
        project_temporal([lambda f=f, p=p: mid[f, spot(p)] for p in range(pieces)],
                         [(0, [qs.at[f]]), (1, [ks.at[f]]), (2, [vs.at[f]])], tokens)
    for f in range(frames - 1):
        for j in away:
            for p in range(pieces):
                m_copies[f, p, j].wait_recv()
            project_temporal([lambda f=f, j=j, p=p: mids[j - 1, f, spot(p)] for p in range(pieces)],
                             [(1, [ks.at[j * frames + f]]), (2, [vs.at[j * frames + f]])], tokens)

    k_order = [order_ref[(t - j) % ranks * frames + g] for j in range(ranks) for g in range(frames)]
    size = max(16, min(PIECE, 256 // (frames * keys)))
    pairs = [(f, g) for f in range(frames) for g in range(keys)]

    def attend_temporal(first, count):
        per = PIECE // size

        def step(i, carry):
            at = pl.ds(pl.multiple_of(first * PIECE + i * size, size), size)
            piece, within = first + i // per, i % per
            q = [qs[f, at] * BF(SCALE) for f in range(frames)]
            products = jnp.concatenate([q[f] * ks[g, at] for f, g in pairs], axis=0)
            scores = jnp.dot(products, gather[...], preferred_element_type=F32)
            scores = {pair: scores[n * size:(n + 1) * size] for n, pair in enumerate(pairs)}
            weights = []
            for f in range(frames):
                kept = [scores[f, g] + jnp.where(k_order[g] <= k_order[f], 0.0, -1e30) for g in range(keys)]
                top_score = functools.reduce(jnp.maximum, kept)
                exps = [jnp.exp(sc - top_score) for sc in kept]
                scale = 1.0 / functools.reduce(jnp.add, exps)
                weights += [(e * scale).astype(BF) for e in exps]
            spreads = jnp.dot(jnp.concatenate(weights, axis=0), spread[...], preferred_element_type=F32)
            for f in range(frames):
                total = None
                for g in range(keys):
                    n = f * keys + g
                    term = spreads[n * size:(n + 1) * size] * vs[g, at].astype(F32)
                    total = term if total is None else total + term
                ctx2[0, piece, f, pl.ds(pl.multiple_of(within * size, size), size)] = total.astype(BF)
            return carry

        lax.fori_loop(0, count * per, step, 0)

    row_tile = 1024
    sub = depth // (ranks * places * ny)
    stacked = frames * PIECE

    def add_gradient(terms, first, final):
        def step(i, carry):
            at = pl.ds(pl.multiple_of(i * row_tile, row_tile), row_tile)
            left = jnp.concatenate([ctx2[w, p, :, :, at].reshape(stacked, row_tile) for w, p in terms], axis=0)
            right = jnp.concatenate([cot[w, p].reshape(stacked, half) for w, p in terms], axis=0)
            got = lax.dot_general(left, right, (((0,), (0,)), ((), ())), preferred_element_type=F32)
            if not first:
                got = got + accf[at]
            if final:
                acc[at] = got.astype(BF)
            else:
                accf[at] = got
            return carry

        lax.fori_loop(0, depth // row_tile, step, 0)

    c_copies = []
    final = frames - 1
    ready(*[f"cot{f}" for f in range(frames)])
    for copy in cot_copies:
        copy.wait()
    per_chunk = span // PIECE
    arrival = [c * per_chunk + i for c in reversed(range(chunks)) for i in range(per_chunk)]
    groups = [arrival[n:n + per_chunk] for n in range(0, pieces - per_chunk, per_chunk)]
    groups += [[p] for p in arrival[-per_chunk:]]
    ahead = []
    for number, group in enumerate(groups):
        for p in group:
            for j in away:
                m_copies[final, p, j].wait_recv()
        lo, n = group[0], len(group)
        whole = slice(lo * PIECE, (lo + n) * PIECE)
        for j in away:
            project_temporal([lambda j=j, p=p: mids[j - 1, final, spot(p)] for p in group],
                             [(1, [ks.at[j * frames + final, whole]]), (2, [vs.at[j * frames + final, whole]])],
                             n * PIECE)
        attend_temporal(lo, n)
        copy = remote(ctx2.at[0, lo:lo + n], ctx2.at[1, lo:lo + n], s_cs.at[frames + number],
                      s_cr.at[frames + number], "batch", other_core)
        copy.start()
        c_copies.append(copy)
        if number:
            c_copies[number - 1].wait_recv()
        add_gradient([(0, p) for p in group] + [(1, p) for p in ahead], number == 0, False)
        ahead = group
    c_copies[-1].wait_recv()
    add_gradient([(1, p) for p in ahead], False, True)

    sems = iter(range(s_gs.shape[0]))

    def exchange(axis, me, count, to_device, source, dests):
        copies = []
        for k in range(1, count):
            to = (me + k) % count
            n = next(sems)
            copy = remote(source(to), dests.at[k - 1], s_gs.at[n], s_gr.at[n], axis, to_device(to))
            copy.start()
            copies.append(copy)
        return copies

    def over_x(source, dests):
        return exchange("tm", t, ranks, lambda to: to, source, dests)

    def over_y(source, dests):
        return exchange("batch", y, ny, lambda to: to * 2 + core, source, dests)

    def over_z(source, dests):
        return exchange("space", s, places, lambda to: to, source, dests)

    def wait(copies):
        for copy in copies:
            copy.wait()

    def total_of(first, received, count):
        total = first.astype(F32)
        for k in range(count - 1):
            total = total + received[k].astype(F32)
        return total

    stage_one = []
    grid = acc.reshape(ranks, places, ny, sub, half)
    column = lambda n: slice(n * LANES, (n + 1) * LANES)
    count = half // LANES
    for n in range(count):
        if n % 2 == 0:
            stage_one.append(over_x(lambda to, n=n: grid.at[to, :, :, :, column(n)], xr_one.at[n // 2]))
        else:
            stage_one.append(over_y(lambda to, n=n: grid.at[:, :, to, :, column(n)], yr_one.at[n // 2]))

    ready("o2")

    def out_step(i, carry):
        at = pl.ds(pl.multiple_of(i * TILE, TILE), TILE)
        got = jnp.dot(ctx2[0].reshape(frames * tokens, depth), o2[:, at], preferred_element_type=F32)
        for p in range(pieces):
            for f in range(frames):
                base = (p * frames + f) * PIECE
                qs[f, spot(p), at] = (mid[f, spot(p), at].astype(F32) + got[base:base + PIECE]).astype(BF)
        return carry

    lax.fori_loop(0, depth // TILE, out_step, 0)
    out_copy = pltpu.make_async_copy(qs, out, s_out)
    out_copy.start()

    stage_two = []
    for n in range(count):
        wait(stage_one[n])
        k = n // 2
        if n % 2 == 0:
            one_x[k] = total_of(grid[t, :, :, :, column(n)], xr_one.at[k], ranks).astype(BF)
            stage_two.append(over_y(lambda to, k=k: one_x.at[k, :, to], yr_two.at[k]))
        else:
            one_y[k] = total_of(grid[:, :, y, :, column(n)], yr_one.at[k], ny).astype(BF)
            stage_two.append(over_x(lambda to, k=k: one_y.at[k, to], xr_two.at[k]))
    stage_three = []
    for n in range(count):
        wait(stage_two[n])
        k = n // 2
        if n % 2 == 0:
            two[n] = total_of(one_x[k, :, y], yr_two.at[k], ny).astype(BF)
        else:
            two[n] = total_of(one_y[k, t], xr_two.at[k], ranks).astype(BF)
        stage_three.append(over_z(lambda to, n=n: two.at[n, to], zr.at[n]))
    for n in range(count):
        wait(stage_three[n])
        gp[:, column(n)] = total_of(two[n, s], zr.at[n], places).astype(BF)
    last = exchange("batch", b, parts, lambda to: to, lambda to: gp, gr)

    def place_piece(owner, value):
        grad[pl.ds(pl.multiple_of(owner // 2 * sub, sub), sub), half_of(owner % 2)] = value.astype(F32)

    place_piece(b, gp[...])
    for k, copy in enumerate(last):
        copy.wait()
        place_piece((b - 1 - k) % parts, gr[k])

    for copies in (x_copies, m_copies):
        for copy in copies.values():
            copy.wait_send()
    for copy in c_copies:
        copy.wait_send()
    for f in range(frames):
        for j in range(ranks):
            finish_halo(f, j)
    out_copy.wait()


def per_device(clip_tokens, frame_order, row_reach, spatial_gain, spatial_heads, spatial_merge,
               temporal_gain, temporal_heads, temporal_merge, cotangent):
    ranks, places, parts = lax.axis_size("tm"), lax.axis_size("space"), lax.axis_size("batch")
    _, all_frames, rows, pc, depth = clip_tokens.shape
    frames, cols = all_frames // ranks, pc * ranks
    chunks, blk, tokens = rows // HALO, HALO * pc, rows * cols
    span = blk * ranks
    keys = ranks * frames
    ny = parts // 2
    half = depth // 2
    sub = depth // (ranks * places * ny)
    pieces = tokens // PIECE
    chunks_of = half // LANES
    pairs = chunks_of // 2
    dims = (ranks, places, parts, frames, chunks, pc, depth)
    anywhere = pl.BlockSpec(memory_space=pl.ANY)
    smem = pl.BlockSpec(memory_space=pltpu.SMEM)
    vmem = pl.BlockSpec(memory_space=pltpu.VMEM)
    dma = pltpu.SemaphoreType.DMA
    others, ny_others = max(ranks - 1, 1), max(ny - 1, 1)
    most = max(frames * chunks * blk, 2 * ranks * blk, (ranks - 1) * max(chunks, 2) * blk,
               tokens)
    steps = pairs * 2 * (ranks - 1) + pairs * 2 * (ny - 1) + chunks_of * (places - 1) + (parts - 1)
    scratch = [
        pltpu.VMEM((frames, chunks + 2, ranks, blk, depth), BF),
        pltpu.VMEM((others, frames, chunks, blk, depth), BF),
        pltpu.VMEM((3, frames, chunks + 2, ranks, blk, depth), BF),
        pltpu.VMEM((most, depth), BF),
        pltpu.VMEM((depth, 3 * depth), BF),
        pltpu.VMEM((depth, depth), BF),
        pltpu.VMEM((depth, 3 * depth), BF),
        pltpu.VMEM((depth, depth), BF),
        pltpu.VMEM((span, depth), BF),
        pltpu.VMEM((frames, tokens, depth), BF),
        pltpu.VMEM((others, frames, tokens, depth), BF),
        pltpu.VMEM((frames, tokens, depth), BF),
        pltpu.VMEM((keys, tokens, depth), BF),
        pltpu.VMEM((keys, tokens, depth), BF),
        pltpu.VMEM((2, pieces, frames, PIECE, depth), BF),
        pltpu.VMEM((2, pieces, frames, PIECE, half), BF),
        pltpu.VMEM((depth, LANES), BF),
        pltpu.VMEM((LANES, depth), BF),
        pltpu.VMEM((frames, chunks, span, 3 * span), F32),
        pltpu.VMEM((depth, half), F32),
        pltpu.VMEM((depth, half), BF),
        pltpu.VMEM((pairs, others, places, ny, sub, LANES), BF),
        pltpu.VMEM((pairs, ny_others, ranks, places, sub, LANES), BF),
        pltpu.VMEM((pairs, places, ny, sub, LANES), BF),
        pltpu.VMEM((pairs, ranks, places, sub, LANES), BF),
        pltpu.VMEM((pairs, others, places, sub, LANES), BF),
        pltpu.VMEM((pairs, ny_others, places, sub, LANES), BF),
        pltpu.VMEM((chunks_of, places, sub, LANES), BF),
        pltpu.VMEM((chunks_of, max(places - 1, 1), sub, LANES), BF),
        pltpu.VMEM((sub, half), BF),
        pltpu.VMEM((parts - 1, sub, half), BF),
        dma((2 * frames + 6 + (ranks - 1) * frames,)),
        dma((frames, chunks, others)), dma((frames, chunks, others)),
        dma((2, frames, ranks)), dma((2, frames, ranks)),
        dma((frames, pieces, others)), dma((frames, pieces, others)),
        dma((frames + pieces,)), dma((frames + pieces,)),
        dma((steps,)), dma((steps,)),
        dma,
    ]
    out, grad = pl.pallas_call(
        functools.partial(block_kernel, dims),
        out_shape=(jax.ShapeDtypeStruct((frames, tokens, depth), BF),
                   jax.ShapeDtypeStruct((ny * sub, depth), F32)),
        in_specs=[anywhere, smem, smem, vmem, vmem] + [anywhere] * 5,
        out_specs=(anywhere, vmem),
        scratch_shapes=scratch,
        compiler_params=pltpu.CompilerParams(collective_id=0, has_side_effects=True,
                                             vmem_limit_bytes=67043328),
        name="block",
    )(clip_tokens.reshape(all_frames, chunks, blk, depth), frame_order.reshape(-1), row_reach.reshape(-1),
      spatial_gain.reshape(1, depth), temporal_gain.reshape(1, depth),
      spatial_heads, spatial_merge, temporal_heads, temporal_merge, cotangent.reshape(frames, pieces, PIECE, depth))
    return out.reshape(1, frames, rows, cols, depth), grad


def solution(mesh):
    in_specs = (
        P("batch", None, "space", "tm", None),
        P("batch", None),
        P("batch", "tm"),
        P(),
        P(),
        P(),
        P(),
        P(),
        P(),
        P("batch", "tm", "space", None, None),
    )
    out_specs = (P("batch", "tm", "space", None, None), P(("tm", "space"), None))
    return jax.shard_map(per_device, mesh=mesh, in_specs=in_specs, out_specs=out_specs, check_vma=False)
```

time: 95 us -> 75.2 us (0.79)
  Pallas kernels: 89.9 us -> 70.1 us
    pallas_call x1, Pallas kernels: 89.9 us -> 70.1 us  [per_device(): pl.pallas_call(functools.partial(block_kernel, dims), out_shape=(jax.Shap...]
where the time goes in v2:
time: 75.2 us; the launch traced here: 74.9 us
  Pallas kernels  70.1 us (93%)
  local copies, waits for them, and re-layouts  4.17 us (6%)
    pallas_call x1, Pallas kernels, per_device(): pl.pallas_call(functools.partial(block_kernel, dims), out_shape=(jax.Shap...  70.1 us
    unnamed x2, local copies, waits for them, and re-layouts  4.17 us

profile of v2, /device:TPU:0, one launch (start us, length us, event | category | flops | bytes accessed | tf_op | source)
XLA Modules:
  0.0 74.9 jit_solution(8944981982936968346)
XLA Ops:
  0.6 70.1 %block.1 = (bf16[2,256,1024]{2,1,0:T(8,128)(2,1)}, f32[128,1024]{1,0:T(8,128)}) custom-call(bf16[4,2,64,1024]{3,2,1,0:T(8,128)(2,1)} %bitcast.7, s32[4]{0:T(128)} %bitcast.12, s32[2]{0:T(128)} %bitcast.13, f32[1,1024]{1,0:T(1,128)} %bitcast.10, f32[1,1024]{1,0:T(1,128)} %bitcast.11, bf16[1024,3072]{1,0:T(8,128)(2,1)} %refs_5_.1, bf16[1024,1024]{1,0:T(8,128)(2,1)} %refs_6_.1, ...), custom_call_target="tpu_custom_call" | custom-call | tf_op jit(solution)/shard_map/block/pallas_call | solution.py:541
  70.8 2.3 %copy.14 = bf16[1,2,8,32,1024]{4,3,2,1,0:T(8,128)(2,1)} copy(bf16[1,2,8,32,1024]{4,3,2,1,0:T(8,128)(2,1)} %bitcast.9) | data formatting | bytes 2097152
  73.0 1.9 %copy.15 = f32[128,1024]{1,0:T(8,128)} copy(f32[128,1024]{1,0:T(8,128)} %get-tuple-element.9) | data formatting | bytes 1048576

commit v3 on v2

--- a/solution.py
+++ b/solution.py
@@ -12,7 +12,6 @@
 HEAD_DIM = 64
 LANES = 128
 TILE = 1024
-PIECE = 64
 UNROLL = 8
 SCALE = HEAD_DIM ** (-0.5)
 FLOOR = 0.5
@@ -22,16 +21,15 @@
 
 
 def block_kernel(dims, *refs):
-    ranks, places, parts, frames, chunks, pc, depth = dims
+    ranks, places, parts, frames, chunks, pc, depth, inner = dims
+    every = (slice(None), slice(None))
     (clip, order_ref, reach_ref, gain_one, gain_two, w_one, m_one, w_two, m_two, cot_in,
      out, grad,
-     xx, away_x, pr, nb, w1, o1, w2, o2, ctx1, mid, mids, qs, ks, vs, ctx2, cot, gather, spread, bias, accf, acc,
-     xr_one, yr_one, one_x, one_y, xr_two, yr_two, two, zr, gp, gr,
-     s_load, s_xs, s_xr, s_zs, s_zr, s_ms, s_mr, s_cs, s_cr, s_gs, s_gr, s_out) = refs
+     xx, away_x, pr, nb, w1, o1, w2, o2, ctx1, mid, mids, qkv, ctx2, cot, gather, spread, bias, accf, acc,
+     xr_one, yr_one, one_x, one_y, xr_two, yr_two, two, zr, gp, gr, sent,
+     s_load, s_xs, s_xr, s_zs, s_zr, s_ms, s_mr, s_ts, s_tr, s_cs, s_cr, s_os, s_or, s_gs, s_gr) = refs
     blk = HALO * pc
     span = blk * ranks
-    cols = pc * ranks
-    tokens = chunks * span
     rows = chunks * HALO
     keys = ranks * frames
     half = depth // 2
@@ -63,13 +61,17 @@
     load("w2", w_two, w2)
     load("o2", m_two, o2)
     for f in range(frames):
-        load(f"cot{f}", cot_in.at[f, :, :, half_of(core)], cot.at[0, :, f])
+        load(f"cot{f}", cot_in.at[f, :, :, t, :, half_of(core)], cot.at[0, :, f])
 
     barrier = pltpu.get_barrier_semaphore()
     for axis, me, count in (("tm", t, ranks), ("space", s, places), ("batch", b, parts)):
         for shift in range(1, count):
             pl.semaphore_signal(barrier, inc=1, device_id={axis: (me + shift) % count}, device_id_type=MESH)
-    pl.semaphore_wait(barrier, ranks + places + parts - 3)
+    other_core = b + 1 - 2 * core
+    for j in range(1, ranks):
+        pl.semaphore_signal(barrier, inc=1, device_id={"tm": (t + j) % ranks, "batch": other_core},
+                            device_id_type=MESH)
+    pl.semaphore_wait(barrier, 2 * ranks + places + parts - 4)
 
     ready(*[f"x{f}" for f in range(frames)], *[f"y{f}{j}" for f in range(frames) for j in range(1, ranks)])
     def remote(src, dst, send, recv, axis, to):
@@ -125,13 +127,27 @@
 
     send_halo(0, 0, True)
     send_halo(0, 0, False)
-    other_core = b + 1 - 2 * core
     cot_copies = []
-    for f in range(frames):
-        copy = remote(cot_in.at[f, :, :, half_of(1 - core)], cot.at[1, :, f], s_cs.at[f], s_cr.at[f],
-                      "batch", other_core)
-        copy.start()
-        cot_copies.append(copy)
+
+    def send_cotangent(chunk, shifts):
+        for j in shifts:
+            to = (t + j) % ranks
+            for which, core_to in ((0, core), (1, 1 - core)):
+                if j == 0 and which == 0:
+                    continue
+                copy = pltpu.make_async_remote_copy(
+                    cot_in.at[:, chunk, :, to, :, half_of(core_to)],
+                    cot.at[which, chunk, j * frames:(j + 1) * frames],
+                    s_ts.at[which, chunk, j], s_tr.at[which, chunk, j],
+                    device_id={"tm": to, "batch": b - core + core_to}, device_id_type=MESH)
+                copy.start()
+                cot_copies.append((chunk, copy))
+
+    order = list(reversed(range(chunks)))
+    for chunk in order:
+        send_cotangent(chunk, range(1))
+    for chunk in order[:-1]:
+        send_cotangent(chunk, range(1, ranks))
 
     @pl.when(s == 0)
     def _():
@@ -173,7 +189,7 @@
                 pr[i // per, f, slot, source, :, lanes] = got[k * blk:(k + 1) * blk]
             return carry
 
-        lax.fori_loop(first * per, 3 * per, step, 0)
+        lax.fori_loop(first * per, 3 * per, step, 0, unroll=True)
 
     own = range(1, chunks + 1)
     ends = (0, chunks + 1)
@@ -207,20 +223,16 @@
             got = jnp.dot(ctx1[...], o1[:, at], preferred_element_type=F32)
             for source in range(ranks):
                 base = source * blk
-                total = (got[base:base + blk] + xx[f, 1 + chunk, source, :, at].astype(F32)).astype(BF)
-                for r in range(HALO):
-                    row = (chunk * HALO + r) * cols + source * pc
-                    mid[f, row:row + pc, at] = total[r * pc:(r + 1) * pc]
+                total = got[base:base + blk] + xx[f, 1 + chunk, source, :, at].astype(F32)
+                mid[(source - t) % ranks, f, chunk, :, at] = total.astype(BF)
             return carry
 
         lax.fori_loop(0, depth // TILE, step, 0)
-        for piece in range(chunk * span // PIECE, (chunk + 1) * span // PIECE):
-            at = slice(piece * PIECE, (piece + 1) * PIECE)
-            for j in away:
-                copy = remote(mid.at[f, at], mids.at[j - 1, f, at], s_ms.at[f, piece, j - 1],
-                              s_mr.at[f, piece, j - 1], "tm", (t + j) % ranks)
-                copy.start()
-                m_copies[f, piece, j] = copy
+        for j in away:
+            copy = remote(mid.at[j, f, chunk], mids.at[j - 1, f, chunk], s_ms.at[f, chunk, j - 1],
+                          s_mr.at[f, chunk, j - 1], "tm", (t + j) % ranks)
+            copy.start()
+            m_copies[f, chunk, j] = copy
 
     ready("w10", "w11", "w12")
     project_spatial([(f, slot, t) for f in range(frames) for slot in own], 0)
@@ -255,84 +267,74 @@
         if f + 1 < frames:
             project_spatial([(f + 1, slot, (t - j) % ranks) for j in away for slot in own], 0)
 
+    for chunk in order[-1:]:
+        send_cotangent(chunk, range(1, ranks))
     head = lax.broadcasted_iota(jnp.int32, (depth, LANES), 0) // HEAD_DIM
     gather[...] = (head == lax.broadcasted_iota(jnp.int32, (depth, LANES), 1)).astype(F32).astype(BF)
     head = lax.broadcasted_iota(jnp.int32, (LANES, depth), 1) // HEAD_DIM
     spread[...] = (head == lax.broadcasted_iota(jnp.int32, (LANES, depth), 0)).astype(F32).astype(BF)
 
-    def project_temporal(sources, parts_of, count):
-        for i, read in enumerate(sources):
-            nb[i * PIECE:(i + 1) * PIECE] = normalize(read(), gain_two)
+    def project_temporal(blocks):
+        for i, (j, f, chunk) in enumerate(blocks):
+            value = mid[0, f, chunk] if j == 0 else mids[j - 1, f, chunk]
+            nb[i * blk:(i + 1) * blk] = normalize(value, gain_two)
+        count = len(blocks) * blk
         per = depth // TILE
 
-        def make(dst, part):
-            def step(i, carry):
-                at = pl.ds(pl.multiple_of(part * depth + i * TILE, TILE), TILE)
-                lanes = pl.ds(pl.multiple_of(i * TILE, TILE), TILE)
-                got = jnp.dot(nb[:len(sources) * PIECE], w2[:, at], preferred_element_type=F32).astype(BF)
-                for k, ref in enumerate(dst):
-                    ref[:, lanes] = got[k * count:(k + 1) * count]
-                return carry
-            return step
-
-        for part, dst in parts_of:
-            lax.fori_loop(0, per, make(dst, part), 0)
-
-    pieces = tokens // PIECE
-    spot = lambda piece: slice(piece * PIECE, (piece + 1) * PIECE)
+        def step(i, carry):
+            at = pl.ds(pl.multiple_of(i * TILE, TILE), TILE)
+            lanes = pl.ds(pl.multiple_of(i % per * TILE, TILE), TILE)
+            got = jnp.dot(nb[:count], w2[:, at], preferred_element_type=F32).astype(BF)
+            for k, (j, f, chunk) in enumerate(blocks):
+                qkv[i // per, chunk, j * frames + f, :, lanes] = got[k * blk:(k + 1) * blk]
+            return carry
+
+        lax.fori_loop(0, 3 * per, step, 0, unroll=True)
+
     ready("w2")
-    for f in range(frames):
-        project_temporal([lambda f=f, p=p: mid[f, spot(p)] for p in range(pieces)],
-                         [(0, [qs.at[f]]), (1, [ks.at[f]]), (2, [vs.at[f]])], tokens)
-    for f in range(frames - 1):
+    project_temporal([(0, f, chunk) for f in range(frames) for chunk in range(chunks)])
+    for f in range(frames):
         for j in away:
-            for p in range(pieces):
-                m_copies[f, p, j].wait_recv()
-            project_temporal([lambda f=f, j=j, p=p: mids[j - 1, f, spot(p)] for p in range(pieces)],
-                             [(1, [ks.at[j * frames + f]]), (2, [vs.at[j * frames + f]])], tokens)
-
-    k_order = [order_ref[(t - j) % ranks * frames + g] for j in range(ranks) for g in range(frames)]
-    size = max(16, min(PIECE, 256 // (frames * keys)))
-    pairs = [(f, g) for f in range(frames) for g in range(keys)]
-
-    def attend_temporal(first, count):
-        per = PIECE // size
-
-        def step(i, carry):
-            at = pl.ds(pl.multiple_of(first * PIECE + i * size, size), size)
-            piece, within = first + i // per, i % per
-            q = [qs[f, at] * BF(SCALE) for f in range(frames)]
-            products = jnp.concatenate([q[f] * ks[g, at] for f, g in pairs], axis=0)
+            for chunk in range(chunks):
+                m_copies[f, chunk, j].wait_recv()
+        project_temporal([(j, f, chunk) for j in away for chunk in range(chunks)])
+
+    def frame_rank(slot):
+        return order_ref[(t - slot // frames) % ranks * frames + slot % frames]
+
+    k_order = [frame_rank(g) for g in range(keys)]
+
+    def attend_temporal(chunk):
+        def step(f, carry):
+            q = qkv[0, chunk, f] * BF(SCALE)
+            products = jnp.concatenate([q * qkv[1, chunk, g] for g in range(keys)], axis=0)
             scores = jnp.dot(products, gather[...], preferred_element_type=F32)
-            scores = {pair: scores[n * size:(n + 1) * size] for n, pair in enumerate(pairs)}
-            weights = []
-            for f in range(frames):
-                kept = [scores[f, g] + jnp.where(k_order[g] <= k_order[f], 0.0, -1e30) for g in range(keys)]
-                top_score = functools.reduce(jnp.maximum, kept)
-                exps = [jnp.exp(sc - top_score) for sc in kept]
-                scale = 1.0 / functools.reduce(jnp.add, exps)
-                weights += [(e * scale).astype(BF) for e in exps]
-            spreads = jnp.dot(jnp.concatenate(weights, axis=0), spread[...], preferred_element_type=F32)
-            for f in range(frames):
-                total = None
-                for g in range(keys):
-                    n = f * keys + g
-                    term = spreads[n * size:(n + 1) * size] * vs[g, at].astype(F32)
-                    total = term if total is None else total + term
-                ctx2[0, piece, f, pl.ds(pl.multiple_of(within * size, size), size)] = total.astype(BF)
+            own_order = frame_rank(f)
+            kept = [scores[g * blk:(g + 1) * blk] + jnp.where(k_order[g] <= own_order, 0.0, -1e30)
+                    for g in range(keys)]
+            top_score = functools.reduce(jnp.maximum, kept)
+            exps = [jnp.exp(sc - top_score) for sc in kept]
+            scale = 1.0 / functools.reduce(jnp.add, exps)
+            weights = jnp.concatenate([(e * scale).astype(BF) for e in exps], axis=0)
+            spreads = jnp.dot(weights, spread[...], preferred_element_type=F32)
+            total = None
+            for g in range(keys):
+                term = spreads[g * blk:(g + 1) * blk] * qkv[2, chunk, g].astype(F32)
+                total = term if total is None else total + term
+            ctx2[0, chunk, f] = total.astype(BF)
             return carry
 
-        lax.fori_loop(0, count * per, step, 0)
+        lax.fori_loop(0, keys, step, 0, unroll=4)
 
     row_tile = 1024
     sub = depth // (ranks * places * ny)
-    stacked = frames * PIECE
+    stacked = keys * blk
 
     def add_gradient(terms, first, final):
         def step(i, carry):
             at = pl.ds(pl.multiple_of(i * row_tile, row_tile), row_tile)
-            left = jnp.concatenate([ctx2[w, p, :, :, at].reshape(stacked, row_tile) for w, p in terms], axis=0)
-            right = jnp.concatenate([cot[w, p].reshape(stacked, half) for w, p in terms], axis=0)
+            left = jnp.concatenate([ctx2[w, c, :, :, at].reshape(stacked, row_tile) for w, c in terms], axis=0)
+            right = jnp.concatenate([cot[w, c].reshape(stacked, half) for w, c in terms], axis=0)
             got = lax.dot_general(left, right, (((0,), (0,)), ((), ())), preferred_element_type=F32)
             if not first:
                 got = got + accf[at]
@@ -344,37 +346,23 @@
 
         lax.fori_loop(0, depth // row_tile, step, 0)
 
-    c_copies = []
-    final = frames - 1
+    c_copies = {}
     ready(*[f"cot{f}" for f in range(frames)])
-    for copy in cot_copies:
-        copy.wait()
-    per_chunk = span // PIECE
-    arrival = [c * per_chunk + i for c in reversed(range(chunks)) for i in range(per_chunk)]
-    groups = [arrival[n:n + per_chunk] for n in range(0, pieces - per_chunk, per_chunk)]
-    groups += [[p] for p in arrival[-per_chunk:]]
-    ahead = []
-    for number, group in enumerate(groups):
-        for p in group:
-            for j in away:
-                m_copies[final, p, j].wait_recv()
-        lo, n = group[0], len(group)
-        whole = slice(lo * PIECE, (lo + n) * PIECE)
-        for j in away:
-            project_temporal([lambda j=j, p=p: mids[j - 1, final, spot(p)] for p in group],
-                             [(1, [ks.at[j * frames + final, whole]]), (2, [vs.at[j * frames + final, whole]])],
-                             n * PIECE)
-        attend_temporal(lo, n)
-        copy = remote(ctx2.at[0, lo:lo + n], ctx2.at[1, lo:lo + n], s_cs.at[frames + number],
-                      s_cr.at[frames + number], "batch", other_core)
-        copy.start()
-        c_copies.append(copy)
-        if number:
-            c_copies[number - 1].wait_recv()
-        add_gradient([(0, p) for p in group] + [(1, p) for p in ahead], number == 0, False)
-        ahead = group
-    c_copies[-1].wait_recv()
-    add_gradient([(1, p) for p in ahead], False, True)
+    before = None
+    for chunk in order:
+        attend_temporal(chunk)
+        c_copies[chunk] = remote(ctx2.at[0, chunk], ctx2.at[1, chunk], s_cs.at[chunk], s_cr.at[chunk],
+                                 "batch", other_core)
+        c_copies[chunk].start()
+        for of, copy in cot_copies:
+            if of == chunk:
+                copy.wait_recv()
+        if before is not None:
+            c_copies[before].wait_recv()
+        add_gradient([(0, chunk)] + ([(1, before)] if before is not None else []), before is None, False)
+        before = chunk
+    c_copies[before].wait_recv()
+    add_gradient([(1, before)], chunks == 0, True)
 
     sems = iter(range(s_gs.shape[0]))
 
@@ -421,16 +409,29 @@
 
     def out_step(i, carry):
         at = pl.ds(pl.multiple_of(i * TILE, TILE), TILE)
-        got = jnp.dot(ctx2[0].reshape(frames * tokens, depth), o2[:, at], preferred_element_type=F32)
-        for p in range(pieces):
-            for f in range(frames):
-                base = (p * frames + f) * PIECE
-                qs[f, spot(p), at] = (mid[f, spot(p), at].astype(F32) + got[base:base + PIECE]).astype(BF)
+        got = jnp.dot(ctx2[0].reshape(chunks * stacked, depth), o2[:, at], preferred_element_type=F32)
+        for chunk in range(chunks):
+            for j in range(ranks):
+                for f in range(frames):
+                    base = (chunk * keys + j * frames + f) * blk
+                    value = mid[0, f, chunk, :, at] if j == 0 else mids[j - 1, f, chunk, :, at]
+                    value = (value.astype(F32) + got[base:base + blk]).astype(BF)
+                    if j == 0:
+                        out[f, chunk, :, t, :, at] = value.reshape(inner + (TILE,))
+                    else:
+                        sent[(j - 1, chunk, f) + every + (at,)] = value.reshape(inner + (TILE,))
         return carry
 
     lax.fori_loop(0, depth // TILE, out_step, 0)
-    out_copy = pltpu.make_async_copy(qs, out, s_out)
-    out_copy.start()
+    out_copies = []
+
+    def return_output():
+        for chunk in range(chunks):
+            for j in away:
+                copy = remote(sent.at[j - 1, chunk], out.at[:, chunk, :, t], s_os.at[chunk, j - 1],
+                              s_or.at[chunk, j - 1], "tm", (t - j) % ranks)
+                copy.start()
+                out_copies.append(copy)
 
     stage_two = []
     for n in range(count):
@@ -442,6 +443,7 @@
         else:
             one_y[k] = total_of(grid[:, :, y, :, column(n)], yr_one.at[k], ny).astype(BF)
             stage_two.append(over_x(lambda to, k=k: one_y.at[k, to], xr_two.at[k]))
+    return_output()
     stage_three = []
     for n in range(count):
         wait(stage_two[n])
@@ -451,28 +453,35 @@
         else:
             two[n] = total_of(one_y[k, t], xr_two.at[k], ranks).astype(BF)
         stage_three.append(over_z(lambda to, n=n: two.at[n, to], zr.at[n]))
+
+    def place_piece(n, owner, value):
+        rows_at = pl.ds(pl.multiple_of(owner // 2 * sub, sub), sub)
+        lanes = pl.ds(pl.multiple_of(owner % 2 * half + n * LANES, LANES), LANES)
+        grad[rows_at, lanes] = value.astype(F32)
+
+    last = []
     for n in range(count):
         wait(stage_three[n])
-        gp[:, column(n)] = total_of(two[n, s], zr.at[n], places).astype(BF)
-    last = exchange("batch", b, parts, lambda to: to, lambda to: gp, gr)
-
-    def place_piece(owner, value):
-        grad[pl.ds(pl.multiple_of(owner // 2 * sub, sub), sub), half_of(owner % 2)] = value.astype(F32)
-
-    place_piece(b, gp[...])
-    for k, copy in enumerate(last):
-        copy.wait()
-        place_piece((b - 1 - k) % parts, gr[k])
-
-    for copies in (x_copies, m_copies):
+        gp[n] = total_of(two[n, s], zr.at[n], places).astype(BF)
+        last.append(exchange("batch", b, parts, lambda to: to, lambda to, n=n: gp.at[n], gr.at[n]))
+        place_piece(n, b, gp[n])
+    for n in range(count):
+        for k, copy in enumerate(last[n]):
+            copy.wait()
+            place_piece(n, (b - 1 - k) % parts, gr[n, k])
+
+    for copy in out_copies:
+        copy.wait_recv()
+    for copies in (x_copies, m_copies, c_copies):
         for copy in copies.values():
             copy.wait_send()
-    for copy in c_copies:
+    for _, copy in cot_copies:
+        copy.wait_send()
+    for copy in out_copies:
         copy.wait_send()
     for f in range(frames):
         for j in range(ranks):
             finish_halo(f, j)
-    out_copy.wait()
 
 
 def per_device(clip_tokens, frame_order, row_reach, spatial_gain, spatial_heads, spatial_merge,
@@ -480,24 +489,24 @@
     ranks, places, parts = lax.axis_size("tm"), lax.axis_size("space"), lax.axis_size("batch")
     _, all_frames, rows, pc, depth = clip_tokens.shape
     frames, cols = all_frames // ranks, pc * ranks
-    chunks, blk, tokens = rows // HALO, HALO * pc, rows * cols
+    chunks, blk = rows // HALO, HALO * pc
     span = blk * ranks
     keys = ranks * frames
     ny = parts // 2
     half = depth // 2
     sub = depth // (ranks * places * ny)
-    pieces = tokens // PIECE
     chunks_of = half // LANES
     pairs = chunks_of // 2
-    dims = (ranks, places, parts, frames, chunks, pc, depth)
+    inner = (HALO, pc) if pc % 16 == 0 else (1, blk)
+    dims = (ranks, places, parts, frames, chunks, pc, depth, inner)
     anywhere = pl.BlockSpec(memory_space=pl.ANY)
     smem = pl.BlockSpec(memory_space=pltpu.SMEM)
     vmem = pl.BlockSpec(memory_space=pltpu.VMEM)
     dma = pltpu.SemaphoreType.DMA
     others, ny_others = max(ranks - 1, 1), max(ny - 1, 1)
     most = max(frames * chunks * blk, 2 * ranks * blk, (ranks - 1) * max(chunks, 2) * blk,
-               tokens)
-    steps = pairs * 2 * (ranks - 1) + pairs * 2 * (ny - 1) + chunks_of * (places - 1) + (parts - 1)
+               (ranks - 1) * chunks * blk)
+    steps = pairs * 2 * (ranks - 1) + pairs * 2 * (ny - 1) + chunks_of * (places - 1) + chunks_of * (parts - 1)
     scratch = [
         pltpu.VMEM((frames, chunks + 2, ranks, blk, depth), BF),
         pltpu.VMEM((others, frames, chunks, blk, depth), BF),
@@ -508,13 +517,11 @@
         pltpu.VMEM((depth, 3 * depth), BF),
         pltpu.VMEM((depth, depth), BF),
         pltpu.VMEM((span, depth), BF),
-        pltpu.VMEM((frames, tokens, depth), BF),
-        pltpu.VMEM((others, frames, tokens, depth), BF),
-        pltpu.VMEM((frames, tokens, depth), BF),
-        pltpu.VMEM((keys, tokens, depth), BF),
-        pltpu.VMEM((keys, tokens, depth), BF),
-        pltpu.VMEM((2, pieces, frames, PIECE, depth), BF),
-        pltpu.VMEM((2, pieces, frames, PIECE, half), BF),
+        pltpu.VMEM((ranks, frames, chunks, blk, depth), BF),
+        pltpu.VMEM((others, frames, chunks, blk, depth), BF),
+        pltpu.VMEM((3, chunks, keys, blk, depth), BF),
+        pltpu.VMEM((2, chunks, keys, blk, depth), BF),
+        pltpu.VMEM((2, chunks, keys) + inner + (half,), BF),
         pltpu.VMEM((depth, LANES), BF),
         pltpu.VMEM((LANES, depth), BF),
         pltpu.VMEM((frames, chunks, span, 3 * span), F32),
@@ -528,29 +535,36 @@
         pltpu.VMEM((pairs, ny_others, places, sub, LANES), BF),
         pltpu.VMEM((chunks_of, places, sub, LANES), BF),
         pltpu.VMEM((chunks_of, max(places - 1, 1), sub, LANES), BF),
-        pltpu.VMEM((sub, half), BF),
-        pltpu.VMEM((parts - 1, sub, half), BF),
+        pltpu.VMEM((chunks_of, sub, LANES), BF),
+        pltpu.VMEM((chunks_of, parts - 1, sub, LANES), BF),
+        pltpu.VMEM((others, chunks, frames) + inner + (depth,), BF),
         dma((2 * frames + 6 + (ranks - 1) * frames,)),
         dma((frames, chunks, others)), dma((frames, chunks, others)),
         dma((2, frames, ranks)), dma((2, frames, ranks)),
-        dma((frames, pieces, others)), dma((frames, pieces, others)),
-        dma((frames + pieces,)), dma((frames + pieces,)),
+        dma((frames, chunks, others)), dma((frames, chunks, others)),
+        dma((2, chunks, ranks)), dma((2, chunks, ranks)),
+        dma((chunks,)), dma((chunks,)),
+        dma((chunks, others)), dma((chunks, others)),
         dma((steps,)), dma((steps,)),
-        dma,
     ]
+    by_columns = cotangent.reshape(frames, chunks, HALO, ranks, pc, depth)
+    if inner[0] == 1:
+        by_columns = by_columns.transpose(0, 1, 3, 2, 4, 5).reshape(frames, chunks, 1, ranks, blk, depth)
     out, grad = pl.pallas_call(
         functools.partial(block_kernel, dims),
-        out_shape=(jax.ShapeDtypeStruct((frames, tokens, depth), BF),
-                   jax.ShapeDtypeStruct((ny * sub, depth), F32)),
+        out_shape=(pltpu.VMEM((frames, chunks, inner[0], ranks, inner[1], depth), BF),
+                   pltpu.VMEM((ny * sub, depth), F32)),
         in_specs=[anywhere, smem, smem, vmem, vmem] + [anywhere] * 5,
-        out_specs=(anywhere, vmem),
+        out_specs=(vmem, vmem),
         scratch_shapes=scratch,
         compiler_params=pltpu.CompilerParams(collective_id=0, has_side_effects=True,
-                                             vmem_limit_bytes=67043328),
+                                             vmem_limit_bytes=60 << 20),
         name="block",
     )(clip_tokens.reshape(all_frames, chunks, blk, depth), frame_order.reshape(-1), row_reach.reshape(-1),
       spatial_gain.reshape(1, depth), temporal_gain.reshape(1, depth),
-      spatial_heads, spatial_merge, temporal_heads, temporal_merge, cotangent.reshape(frames, pieces, PIECE, depth))
+      spatial_heads, spatial_merge, temporal_heads, temporal_merge, by_columns)
+    if inner[0] == 1:
+        out = out.reshape(frames, chunks, ranks, HALO, pc, depth).transpose(0, 1, 3, 2, 4, 5)
     return out.reshape(1, frames, rows, cols, depth), grad
 
 

time: 75.2 us -> 69.6 us (0.926)
  Pallas kernels: 70.1 us -> 67 us
  local copies, waits for them, and re-layouts: 4.17 us -> 1.77 us
    pallas_call x1, Pallas kernels: 70.1 us -> 67 us  [per_device(): pl.pallas_call(functools.partial(block_kernel, dims), out_shape=(pltpu.VM...]
    unnamed x2, local copies, waits for them, and re-layouts: 4.17 us -> 1.77 us
where the time goes in v3:
time: 69.6 us; the launch traced here: 69.4 us
  Pallas kernels  67 us (96%)
  local copies, waits for them, and re-layouts  1.77 us (3%)
    pallas_call x1, Pallas kernels, per_device(): pl.pallas_call(functools.partial(block_kernel, dims), out_shape=(pltpu.VM...  67 us
    unnamed x2, local copies, waits for them, and re-layouts  1.77 us

profile of v3, /device:TPU:0, one launch (start us, length us, event | category | flops | bytes accessed | tf_op | source)
XLA Modules:
  0.0 69.4 jit_solution(2531022456707250898)
XLA Ops:
  0.6 67.0 %block.1 = (bf16[2,2,4,2,16,1024]{5,4,3,2,1,0:T(8,128)(2,1)S(1)}, f32[128,1024]{1,0:T(8,128)S(1)}) custom-call(bf16[4,2,64,1024]{3,2,1,0:T(8,128)(2,1)} %bitcast.8, s32[4]{0:T(128)} %bitcast.12, s32[2]{0:T(128)} %bitcast.13, f32[1,1024]{1,0:T(1,128)} %bitcast.10, f32[1,1024]{1,0:T(1,128)} %bitcast.11, bf16[1024,3072]{1,0:T(8,128)(2,1)} %refs_5_.1, ...), custom_call_target="tpu_custom_call" | custom-call | tf_op jit(solution)/shard_map/block/pallas_call | solution.py:553
  67.7 1.0 %copy.14 = bf16[1,2,8,32,1024]{4,3,2,1,0:T(8,128)(2,1)} copy(bf16[1,2,8,32,1024]{4,3,2,1,0:T(8,128)(2,1)S(1)} %bitcast.7) | data formatting | bytes 2097152
  68.6 0.8 %copy.15 = f32[128,1024]{1,0:T(8,128)} copy(f32[128,1024]{1,0:T(8,128)S(1)} %get-tuple-element.7) | data formatting | bytes 1048576

commit v4 on v3

--- a/solution.py
+++ b/solution.py
@@ -13,6 +13,8 @@
 LANES = 128
 TILE = 1024
 UNROLL = 8
+ROUTES = ("xyz", "yxz", "zxy", "yxz")
+WAITS = ((0, 0), (1, 0), (3, 0), (1, 1), (0, 1), (2, 0), (3, 1), (2, 1), (0, 2), (1, 2), (2, 2), (3, 2))
 SCALE = HEAD_DIM ** (-0.5)
 FLOOR = 0.5
 BF = jnp.bfloat16
@@ -26,8 +28,9 @@
     (clip, order_ref, reach_ref, gain_one, gain_two, w_one, m_one, w_two, m_two, cot_in,
      out, grad,
      xx, away_x, pr, nb, w1, o1, w2, o2, ctx1, mid, mids, qkv, ctx2, cot, gather, spread, bias, accf, acc,
-     xr_one, yr_one, one_x, one_y, xr_two, yr_two, two, zr, gp, gr, sent,
-     s_load, s_xs, s_xr, s_zs, s_zr, s_ms, s_mr, s_ts, s_tr, s_cs, s_cr, s_os, s_or, s_gs, s_gr) = refs
+     gr, sent, *rest) = refs
+    arrived, summed = rest[:3 * len(ROUTES)], rest[3 * len(ROUTES):6 * len(ROUTES)]
+    (s_load, s_xs, s_xr, s_zs, s_zr, s_ms, s_mr, s_ts, s_tr, s_cs, s_cr, s_os, s_or, s_gs, s_gr) = rest[6 * len(ROUTES):]
     blk = HALO * pc
     span = blk * ranks
     rows = chunks * HALO
@@ -293,7 +296,8 @@
 
     ready("w2")
     project_temporal([(0, f, chunk) for f in range(frames) for chunk in range(chunks)])
-    for f in range(frames):
+    final = frames - 1
+    for f in range(final):
         for j in away:
             for chunk in range(chunks):
                 m_copies[f, chunk, j].wait_recv()
@@ -346,10 +350,36 @@
 
         lax.fori_loop(0, depth // row_tile, step, 0)
 
+    def merge_temporal(chunk):
+        got = jnp.dot(ctx2[0, chunk].reshape(stacked, depth), o2[...], preferred_element_type=F32)
+        for j in range(ranks):
+            for f in range(frames):
+                base = (j * frames + f) * blk
+                value = mid[0, f, chunk] if j == 0 else mids[j - 1, f, chunk]
+                value = (value.astype(F32) + got[base:base + blk]).astype(BF).reshape(inner + (depth,))
+                if j == 0:
+                    out[f, chunk, :, t] = value
+                else:
+                    sent[j - 1, chunk, f] = value
+
+    out_copies = []
+    returns = {chunk: [(chunk, f, j) for f in range(frames) for j in away] for chunk in order}
+
+    def return_output(some):
+        for chunk, f, j in some:
+            copy = remote(sent.at[j - 1, chunk, f], out.at[f, chunk, :, t], s_os.at[chunk, f, j - 1],
+                          s_or.at[chunk, f, j - 1], "tm", (t - j) % ranks)
+            copy.start()
+            out_copies.append(copy)
+
     c_copies = {}
     ready(*[f"cot{f}" for f in range(frames)])
+    ready("o2")
     before = None
     for chunk in order:
+        for j in away:
+            m_copies[final, chunk, j].wait_recv()
+        project_temporal([(j, final, chunk) for j in away])
         attend_temporal(chunk)
         c_copies[chunk] = remote(ctx2.at[0, chunk], ctx2.at[1, chunk], s_cs.at[chunk], s_cr.at[chunk],
                                  "batch", other_core)
@@ -360,112 +390,86 @@
         if before is not None:
             c_copies[before].wait_recv()
         add_gradient([(0, chunk)] + ([(1, before)] if before is not None else []), before is None, False)
+        if chunk != order[-1]:
+            merge_temporal(chunk)
+            return_output(returns[chunk][:len(returns[chunk]) // 2])
         before = chunk
     c_copies[before].wait_recv()
     add_gradient([(1, before)], chunks == 0, True)
 
     sems = iter(range(s_gs.shape[0]))
-
-    def exchange(axis, me, count, to_device, source, dests):
+    axes = {"x": ("tm", t, ranks, lambda to: to), "z": ("space", s, places, lambda to: to),
+            "y": ("batch", y, ny, lambda to: to * 2 + core)}
+    column = lambda n: slice(n * LANES, (n + 1) * LANES)
+    count = half // LANES
+    grid = acc.reshape(ranks, places, ny, sub, half)
+
+    def exchange(axis, source, dests):
+        name, me, size, device = axes[axis]
         copies = []
-        for k in range(1, count):
-            to = (me + k) % count
+        for k in range(1, size):
+            to = (me + k) % size
             n = next(sems)
-            copy = remote(source(to), dests.at[k - 1], s_gs.at[n], s_gr.at[n], axis, to_device(to))
+            copy = remote(source(to), dests.at[k - 1], s_gs.at[n], s_gr.at[n], name, device(to))
             copy.start()
             copies.append(copy)
         return copies
 
-    def over_x(source, dests):
-        return exchange("tm", t, ranks, lambda to: to, source, dests)
-
-    def over_y(source, dests):
-        return exchange("batch", y, ny, lambda to: to * 2 + core, source, dests)
-
-    def over_z(source, dests):
-        return exchange("space", s, places, lambda to: to, source, dests)
-
-    def wait(copies):
-        for copy in copies:
+    def place_in(n, stage, value):
+        route = ROUTES[n]
+        left = [a for a in "xzy" if a not in route[:stage]]
+        at = tuple(value if a == route[stage] else slice(None) for a in left)
+        return at + (slice(None), column(n)) if stage == 0 else at
+
+    flying = {}
+
+    def launch(n, stage):
+        src = grid if stage == 0 else summed[3 * n + stage - 1]
+        flying[n, stage] = exchange(ROUTES[n][stage], lambda to: src.at[place_in(n, stage, to)],
+                                    arrived[3 * n + stage])
+
+    def finish(n, stage):
+        for copy in flying[n, stage]:
             copy.wait()
-
-    def total_of(first, received, count):
-        total = first.astype(F32)
-        for k in range(count - 1):
-            total = total + received[k].astype(F32)
-        return total
-
-    stage_one = []
-    grid = acc.reshape(ranks, places, ny, sub, half)
-    column = lambda n: slice(n * LANES, (n + 1) * LANES)
-    count = half // LANES
-    for n in range(count):
-        if n % 2 == 0:
-            stage_one.append(over_x(lambda to, n=n: grid.at[to, :, :, :, column(n)], xr_one.at[n // 2]))
-        else:
-            stage_one.append(over_y(lambda to, n=n: grid.at[:, :, to, :, column(n)], yr_one.at[n // 2]))
-
-    ready("o2")
-
-    def out_step(i, carry):
-        at = pl.ds(pl.multiple_of(i * TILE, TILE), TILE)
-        got = jnp.dot(ctx2[0].reshape(chunks * stacked, depth), o2[:, at], preferred_element_type=F32)
-        for chunk in range(chunks):
-            for j in range(ranks):
-                for f in range(frames):
-                    base = (chunk * keys + j * frames + f) * blk
-                    value = mid[0, f, chunk, :, at] if j == 0 else mids[j - 1, f, chunk, :, at]
-                    value = (value.astype(F32) + got[base:base + blk]).astype(BF)
-                    if j == 0:
-                        out[f, chunk, :, t, :, at] = value.reshape(inner + (TILE,))
-                    else:
-                        sent[(j - 1, chunk, f) + every + (at,)] = value.reshape(inner + (TILE,))
-        return carry
-
-    lax.fori_loop(0, depth // TILE, out_step, 0)
-    out_copies = []
-
-    def return_output():
-        for chunk in range(chunks):
-            for j in away:
-                copy = remote(sent.at[j - 1, chunk], out.at[:, chunk, :, t], s_os.at[chunk, j - 1],
-                              s_or.at[chunk, j - 1], "tm", (t - j) % ranks)
-                copy.start()
-                out_copies.append(copy)
-
-    stage_two = []
-    for n in range(count):
-        wait(stage_one[n])
-        k = n // 2
-        if n % 2 == 0:
-            one_x[k] = total_of(grid[t, :, :, :, column(n)], xr_one.at[k], ranks).astype(BF)
-            stage_two.append(over_y(lambda to, k=k: one_x.at[k, :, to], yr_two.at[k]))
-        else:
-            one_y[k] = total_of(grid[:, :, y, :, column(n)], yr_one.at[k], ny).astype(BF)
-            stage_two.append(over_x(lambda to, k=k: one_y.at[k, to], xr_two.at[k]))
-    return_output()
-    stage_three = []
-    for n in range(count):
-        wait(stage_two[n])
-        k = n // 2
-        if n % 2 == 0:
-            two[n] = total_of(one_x[k, :, y], yr_two.at[k], ny).astype(BF)
-        else:
-            two[n] = total_of(one_y[k, t], xr_two.at[k], ranks).astype(BF)
-        stage_three.append(over_z(lambda to, n=n: two.at[n, to], zr.at[n]))
+        src = grid if stage == 0 else summed[3 * n + stage - 1]
+        _, me, size, _ = axes[ROUTES[n][stage]]
+        total = src[place_in(n, stage, me)].astype(F32)
+        for k in range(size - 1):
+            total = total + arrived[3 * n + stage][k].astype(F32)
+        summed[3 * n + stage][...] = total.astype(BF)
+        if stage < 2:
+            launch(n, stage + 1)
 
     def place_piece(n, owner, value):
         rows_at = pl.ds(pl.multiple_of(owner // 2 * sub, sub), sub)
         lanes = pl.ds(pl.multiple_of(owner % 2 * half + n * LANES, LANES), LANES)
         grad[rows_at, lanes] = value.astype(F32)
 
-    last = []
+    last = {}
+
+    def gather_piece(n):
+        piece = summed[3 * n + 2]
+        last[n] = []
+        for k in range(1, parts):
+            at = next(sems)
+            copy = remote(piece, gr.at[n, k - 1], s_gs.at[at], s_gr.at[at], "batch", (b + k) % parts)
+            copy.start()
+            last[n].append(copy)
+        place_piece(n, b, piece[...])
+
     for n in range(count):
-        wait(stage_three[n])
-        gp[n] = total_of(two[n, s], zr.at[n], places).astype(BF)
-        last.append(exchange("batch", b, parts, lambda to: to, lambda to, n=n: gp.at[n], gr.at[n]))
-        place_piece(n, b, gp[n])
-    for n in range(count):
+        launch(n, 0)
+
+    for chunk in order[:-1]:
+        return_output(returns[chunk][len(returns[chunk]) // 2:])
+    merge_temporal(order[-1])
+    for n, stage in WAITS:
+        finish(n, stage)
+        if (n, stage) == (2, 0):
+            return_output(returns[order[-1]])
+        if stage == 2:
+            gather_piece(n)
+    for n in last:
         for k, copy in enumerate(last[n]):
             copy.wait()
             place_piece(n, (b - 1 - k) % parts, gr[n, k])
@@ -496,17 +500,24 @@
     half = depth // 2
     sub = depth // (ranks * places * ny)
     chunks_of = half // LANES
-    pairs = chunks_of // 2
     inner = (HALO, pc) if pc % 16 == 0 else (1, blk)
     dims = (ranks, places, parts, frames, chunks, pc, depth, inner)
     anywhere = pl.BlockSpec(memory_space=pl.ANY)
     smem = pl.BlockSpec(memory_space=pltpu.SMEM)
     vmem = pl.BlockSpec(memory_space=pltpu.VMEM)
     dma = pltpu.SemaphoreType.DMA
-    others, ny_others = max(ranks - 1, 1), max(ny - 1, 1)
+    others = max(ranks - 1, 1)
     most = max(frames * chunks * blk, 2 * ranks * blk, (ranks - 1) * max(chunks, 2) * blk,
                (ranks - 1) * chunks * blk)
-    steps = pairs * 2 * (ranks - 1) + pairs * 2 * (ny - 1) + chunks_of * (places - 1) + chunks_of * (parts - 1)
+    sizes = {"x": ranks, "z": places, "y": ny}
+    arrivals, sums, steps = [], [], 0
+    for route in ROUTES:
+        for stage in range(3):
+            left = tuple(sizes[a] for a in "xzy" if a not in route[:stage + 1])
+            arrivals.append(pltpu.VMEM((max(sizes[route[stage]] - 1, 1),) + left + (sub, LANES), BF))
+            sums.append(pltpu.VMEM(left + (sub, LANES), BF))
+            steps += sizes[route[stage]] - 1
+        steps += parts - 1
     scratch = [
         pltpu.VMEM((frames, chunks + 2, ranks, blk, depth), BF),
         pltpu.VMEM((others, frames, chunks, blk, depth), BF),
@@ -527,24 +538,16 @@
         pltpu.VMEM((frames, chunks, span, 3 * span), F32),
         pltpu.VMEM((depth, half), F32),
         pltpu.VMEM((depth, half), BF),
-        pltpu.VMEM((pairs, others, places, ny, sub, LANES), BF),
-        pltpu.VMEM((pairs, ny_others, ranks, places, sub, LANES), BF),
-        pltpu.VMEM((pairs, places, ny, sub, LANES), BF),
-        pltpu.VMEM((pairs, ranks, places, sub, LANES), BF),
-        pltpu.VMEM((pairs, others, places, sub, LANES), BF),
-        pltpu.VMEM((pairs, ny_others, places, sub, LANES), BF),
-        pltpu.VMEM((chunks_of, places, sub, LANES), BF),
-        pltpu.VMEM((chunks_of, max(places - 1, 1), sub, LANES), BF),
-        pltpu.VMEM((chunks_of, sub, LANES), BF),
         pltpu.VMEM((chunks_of, parts - 1, sub, LANES), BF),
         pltpu.VMEM((others, chunks, frames) + inner + (depth,), BF),
+        *arrivals, *sums,
         dma((2 * frames + 6 + (ranks - 1) * frames,)),
         dma((frames, chunks, others)), dma((frames, chunks, others)),
         dma((2, frames, ranks)), dma((2, frames, ranks)),
         dma((frames, chunks, others)), dma((frames, chunks, others)),
         dma((2, chunks, ranks)), dma((2, chunks, ranks)),
         dma((chunks,)), dma((chunks,)),
-        dma((chunks, others)), dma((chunks, others)),
+        dma((chunks, frames, others)), dma((chunks, frames, others)),
         dma((steps,)), dma((steps,)),
     ]
     by_columns = cotangent.reshape(frames, chunks, HALO, ranks, pc, depth)

time: 69.6 us -> 64.9 us (0.932)
  Pallas kernels: 67 us -> 62.3 us
    pallas_call x1, Pallas kernels: 67 us -> 62.3 us  [per_device(): pl.pallas_call(functools.partial(block_kernel, dims), out_shape=(pltpu.VM...]
where the time goes in v4:
time: 64.9 us; the launch traced here: 64.7 us
  Pallas kernels  62.3 us (96%)
  local copies, waits for them, and re-layouts  1.77 us (3%)
    pallas_call x1, Pallas kernels, per_device(): pl.pallas_call(functools.partial(block_kernel, dims), out_shape=(pltpu.VM...  62.3 us
    unnamed x2, local copies, waits for them, and re-layouts  1.77 us

profile of v4, /device:TPU:0, one launch (start us, length us, event | category | flops | bytes accessed | tf_op | source)
XLA Modules:
  0.0 64.7 jit_solution(8572792453865409860)
XLA Ops:
  0.6 62.3 %block.1 = (bf16[2,2,4,2,16,1024]{5,4,3,2,1,0:T(8,128)(2,1)S(1)}, f32[128,1024]{1,0:T(8,128)S(1)}) custom-call(bf16[4,2,64,1024]{3,2,1,0:T(8,128)(2,1)} %bitcast.8, s32[4]{0:T(128)} %bitcast.12, s32[2]{0:T(128)} %bitcast.13, f32[1,1024]{1,0:T(1,128)} %bitcast.10, f32[1,1024]{1,0:T(1,128)} %bitcast.11, bf16[1024,3072]{1,0:T(8,128)(2,1)} %refs_5_.1, ...), custom_call_target="tpu_custom_call" | custom-call | tf_op jit(solution)/shard_map/block/pallas_call | solution.py:556
  63.0 1.0 %copy.14 = bf16[1,2,8,32,1024]{4,3,2,1,0:T(8,128)(2,1)} copy(bf16[1,2,8,32,1024]{4,3,2,1,0:T(8,128)(2,1)S(1)} %bitcast.7) | data formatting | bytes 2097152
  63.9 0.8 %copy.15 = f32[128,1024]{1,0:T(8,128)} copy(f32[128,1024]{1,0:T(8,128)S(1)} %get-tuple-element.7) | data formatting | bytes 1048576

commit v5 on v4

--- a/solution.py
+++ b/solution.py
@@ -25,10 +25,10 @@
 def block_kernel(dims, *refs):
     ranks, places, parts, frames, chunks, pc, depth, inner = dims
     every = (slice(None), slice(None))
-    (clip, order_ref, reach_ref, gain_one, gain_two, w_one, m_one, w_two, m_two, cot_in,
+    (clip, order_in, reach_in, gain_one_in, gain_two_in, w_one, m_one, w_two, m_two, cot_in,
      out, grad,
      xx, away_x, pr, nb, w1, o1, w2, o2, ctx1, mid, mids, qkv, ctx2, cot, gather, spread, bias, accf, acc,
-     gr, sent, *rest) = refs
+     gr, sent, order_ref, reach_ref, gain_one, gain_two, *rest) = refs
     arrived, summed = rest[:3 * len(ROUTES)], rest[3 * len(ROUTES):6 * len(ROUTES)]
     (s_load, s_xs, s_xr, s_zs, s_zr, s_ms, s_mr, s_ts, s_tr, s_cs, s_cr, s_os, s_or, s_gs, s_gr) = rest[6 * len(ROUTES):]
     blk = HALO * pc
@@ -58,6 +58,9 @@
         load(f"x{f}", clip.at[t * frames + f], xx.at[f, 1:chunks + 1, t])
         for j in range(1, ranks):
             load(f"y{f}{j}", clip.at[(t + j) % ranks * frames + f], away_x.at[j - 1, f])
+    for name, src, dst in (("reach", reach_in, reach_ref), ("order", order_in, order_ref),
+                           ("gain1", gain_one_in, gain_one), ("gain2", gain_two_in, gain_two)):
+        load(name, src, dst)
     for part in range(3):
         load(f"w1{part}", w_one.at[:, part * depth:(part + 1) * depth], w1.at[:, part * depth:(part + 1) * depth])
     load("o1", m_one, o1)
@@ -160,6 +163,7 @@
     def _():
         xx[:, chunks + 1] = jnp.zeros((frames, ranks, blk, depth), BF)
 
+    ready("reach", "gain1")
     lane = lax.broadcasted_iota(jnp.int32, (1, LANES), 1)
     first_head = (lane < HEAD_DIM).astype(F32)
     masks = (first_head.astype(BF), (1.0 - first_head).astype(BF))
@@ -255,18 +259,18 @@
             for j in range(ranks):
                 wait_halo(f, j)
             project_spatial([(f, slot, (t - j) % ranks) for j in range(ranks) for slot in ends], 1)
-        if f + 1 < frames:
-            for chunk in range(chunks - 1):
-                forward(f + 1, chunk)
         for chunk in reversed(range(chunks)):
             if f == 0 and chunk == 0:
                 for j in away:
                     wait_halo(f, j, (False,))
                 project_spatial([(f, 0, (t - j) % ranks) for j in away], 1)
+            if f + 1 < frames and chunk == 0:
+                forward(f + 1, chunks - 1)
             attend_spatial(f, chunk)
+            if f + 1 < frames and chunk == chunks - 1:
+                for early in range(chunks - 1):
+                    forward(f + 1, early)
             merge_spatial(f, chunk)
-            if f + 1 < frames and chunk == chunks - 1:
-                forward(f + 1, chunks - 1)
         if f + 1 < frames:
             project_spatial([(f + 1, slot, (t - j) % ranks) for j in away for slot in own], 0)
 
@@ -294,7 +298,7 @@
 
         lax.fori_loop(0, 3 * per, step, 0, unroll=True)
 
-    ready("w2")
+    ready("w2", "order", "gain2")
     project_temporal([(0, f, chunk) for f in range(frames) for chunk in range(chunks)])
     final = frames - 1
     for f in range(final):
@@ -488,6 +492,14 @@
             finish_halo(f, j)
 
 
+def write_kernel(out_v, grad_v, out, grad, sems):
+    copies = [pltpu.make_async_copy(out_v, out, sems.at[0]), pltpu.make_async_copy(grad_v, grad, sems.at[1])]
+    for copy in copies:
+        copy.start()
+    for copy in copies:
+        copy.wait()
+
+
 def per_device(clip_tokens, frame_order, row_reach, spatial_gain, spatial_heads, spatial_merge,
                temporal_gain, temporal_heads, temporal_merge, cotangent):
     ranks, places, parts = lax.axis_size("tm"), lax.axis_size("space"), lax.axis_size("batch")
@@ -503,7 +515,6 @@
     inner = (HALO, pc) if pc % 16 == 0 else (1, blk)
     dims = (ranks, places, parts, frames, chunks, pc, depth, inner)
     anywhere = pl.BlockSpec(memory_space=pl.ANY)
-    smem = pl.BlockSpec(memory_space=pltpu.SMEM)
     vmem = pl.BlockSpec(memory_space=pltpu.VMEM)
     dma = pltpu.SemaphoreType.DMA
     others = max(ranks - 1, 1)
@@ -540,8 +551,12 @@
         pltpu.VMEM((depth, half), BF),
         pltpu.VMEM((chunks_of, parts - 1, sub, LANES), BF),
         pltpu.VMEM((others, chunks, frames) + inner + (depth,), BF),
+        pltpu.SMEM((all_frames,), jnp.int32),
+        pltpu.SMEM((frames,), jnp.int32),
+        pltpu.VMEM((1, depth), F32),
+        pltpu.VMEM((1, depth), F32),
         *arrivals, *sums,
-        dma((2 * frames + 6 + (ranks - 1) * frames,)),
+        dma((2 * frames + 10 + (ranks - 1) * frames,)),
         dma((frames, chunks, others)), dma((frames, chunks, others)),
         dma((2, frames, ranks)), dma((2, frames, ranks)),
         dma((frames, chunks, others)), dma((frames, chunks, others)),
@@ -557,7 +572,7 @@
         functools.partial(block_kernel, dims),
         out_shape=(pltpu.VMEM((frames, chunks, inner[0], ranks, inner[1], depth), BF),
                    pltpu.VMEM((ny * sub, depth), F32)),
-        in_specs=[anywhere, smem, smem, vmem, vmem] + [anywhere] * 5,
+        in_specs=[anywhere] * 10,
         out_specs=(vmem, vmem),
         scratch_shapes=scratch,
         compiler_params=pltpu.CompilerParams(collective_id=0, has_side_effects=True,
@@ -566,6 +581,14 @@
     )(clip_tokens.reshape(all_frames, chunks, blk, depth), frame_order.reshape(-1), row_reach.reshape(-1),
       spatial_gain.reshape(1, depth), temporal_gain.reshape(1, depth),
       spatial_heads, spatial_merge, temporal_heads, temporal_merge, by_columns)
+    out, grad = pl.pallas_call(
+        write_kernel,
+        out_shape=(jax.ShapeDtypeStruct(out.shape, BF), jax.ShapeDtypeStruct(grad.shape, F32)),
+        in_specs=[vmem, vmem],
+        out_specs=(anywhere, anywhere),
+        scratch_shapes=[dma((2,))],
+        name="write",
+    )(pltpu.with_memory_space_constraint(out, pltpu.VMEM), pltpu.with_memory_space_constraint(grad, pltpu.VMEM))
     if inner[0] == 1:
         out = out.reshape(frames, chunks, ranks, HALO, pc, depth).transpose(0, 1, 3, 2, 4, 5)
     return out.reshape(1, frames, rows, cols, depth), grad

time: 64.9 us -> 63.8 us (0.983)
  local copies, waits for them, and re-layouts: 1.77 us -> 0 us
    unnamed x2 -> x0, local copies, waits for them, and re-layouts: 1.77 us -> none
    pallas_call x0 -> x1, Pallas kernels: none -> 1.16 us  [per_device(): pl.pallas_call(write_kernel, out_shape=(jax.ShapeDtypeStruct(out.shape, B...]
    pallas_call x1, Pallas kernels: 62.3 us -> 61.7 us  [per_device(): pl.pallas_call(functools.partial(block_kernel, dims), out_shape=(pltpu.VM...]
where the time goes in v5:
time: 63.8 us; the launch traced here: 63.6 us
  Pallas kernels  62.8 us (98%)
  between operations  0.8 us (1%)
    pallas_call x1, Pallas kernels, per_device(): pl.pallas_call(functools.partial(block_kernel, dims), out_shape=(pltpu.VM...  61.7 us

profile of v5, /device:TPU:0, one launch (start us, length us, event | category | flops | bytes accessed | tf_op | source)
XLA Modules:
  0.0 63.6 jit_solution(14614920097062603744)
XLA Ops:
  0.6 61.7 %block.1 = (bf16[2,2,4,2,16,1024]{5,4,3,2,1,0:T(8,128)(2,1)S(1)}, f32[128,1024]{1,0:T(8,128)S(1)}) custom-call(bf16[4,2,64,1024]{3,2,1,0:T(8,128)(2,1)} %bitcast.7, s32[4]{0:T(128)} %bitcast.11, s32[2]{0:T(128)} %bitcast.12, f32[1,1024]{1,0:T(1,128)} %bitcast.9, f32[1,1024]{1,0:T(1,128)} %bitcast.10, bf16[1024,3072]{1,0:T(8,128)(2,1)} %refs_5_.1, ...), custom_call_target="tpu_custom_call" | custom-call | tf_op jit(solution)/shard_map/block/pallas_call | solution.py:571
  62.3 1.2 %write.1 = (bf16[2,2,4,2,16,1024]{5,4,3,2,1,0:T(8,128)(2,1)}, f32[128,1024]{1,0:T(8,128)}) custom-call(bf16[2,2,4,2,16,1024]{5,4,3,2,1,0:T(8,128)(2,1)S(1)} %get-tuple-element.6.out_v, f32[128,1024]{1,0:T(8,128)S(1)} %get-tuple-element.7.grad_v), custom_call_target="tpu_custom_call" | custom-call | tf_op jit(solution)/shard_map/write/pallas_call | solution.py:584

commit v6 on v5

--- a/solution.py
+++ b/solution.py
@@ -493,7 +493,11 @@
 
 
 def write_kernel(out_v, grad_v, out, grad, sems):
-    copies = [pltpu.make_async_copy(out_v, out, sems.at[0]), pltpu.make_async_copy(grad_v, grad, sems.at[1])]
+    frames, chunks = out_v.shape[:2]
+    copies = [pltpu.make_async_copy(grad_v, grad, sems.at[frames * chunks])]
+    for f in range(frames):
+        for chunk in range(chunks):
+            copies.append(pltpu.make_async_copy(out_v.at[f, chunk], out.at[f, chunk], sems.at[f * chunks + chunk]))
     for copy in copies:
         copy.start()
     for copy in copies:
@@ -586,7 +590,7 @@
         out_shape=(jax.ShapeDtypeStruct(out.shape, BF), jax.ShapeDtypeStruct(grad.shape, F32)),
         in_specs=[vmem, vmem],
         out_specs=(anywhere, anywhere),
-        scratch_shapes=[dma((2,))],
+        scratch_shapes=[dma((frames * chunks + 1,))],
         name="write",
     )(pltpu.with_memory_space_constraint(out, pltpu.VMEM), pltpu.with_memory_space_constraint(grad, pltpu.VMEM))
     if inner[0] == 1:

time: 63.8 us -> 63.8 us (level)
  no operation moved by 1% of the time
where the time goes in v6:
time: 63.8 us; the launch traced here: 63.6 us
  Pallas kernels  62.8 us (98%)
  between operations  0.8 us (1%)
    pallas_call x1, Pallas kernels, per_device(): pl.pallas_call(functools.partial(block_kernel, dims), out_shape=(pltpu.VM...  61.7 us

profile of v6, /device:TPU:0, one launch (start us, length us, event | category | flops | bytes accessed | tf_op | source)
XLA Modules:
  0.0 63.6 jit_solution(7521751284097306080)
XLA Ops:
  0.6 61.7 %block.1 = (bf16[2,2,4,2,16,1024]{5,4,3,2,1,0:T(8,128)(2,1)S(1)}, f32[128,1024]{1,0:T(8,128)S(1)}) custom-call(bf16[4,2,64,1024]{3,2,1,0:T(8,128)(2,1)} %bitcast.7, s32[4]{0:T(128)} %bitcast.11, s32[2]{0:T(128)} %bitcast.12, f32[1,1024]{1,0:T(1,128)} %bitcast.9, f32[1,1024]{1,0:T(1,128)} %bitcast.10, bf16[1024,3072]{1,0:T(8,128)(2,1)} %refs_5_.1, ...), custom_call_target="tpu_custom_call" | custom-call | tf_op jit(solution)/shard_map/block/pallas_call | solution.py:575
  62.3 1.2 %write.1 = (bf16[2,2,4,2,16,1024]{5,4,3,2,1,0:T(8,128)(2,1)}, f32[128,1024]{1,0:T(8,128)}) custom-call(bf16[2,2,4,2,16,1024]{5,4,3,2,1,0:T(8,128)(2,1)S(1)} %get-tuple-element.6.out_v, f32[128,1024]{1,0:T(8,128)S(1)} %get-tuple-element.7.grad_v), custom_call_target="tpu_custom_call" | custom-call | tf_op jit(solution)/shard_map/write/pallas_call | solution.py:588
